TPU v7x, 256 devices: a 8x8x2 block of a 8x8x16 slice. The times are simulated.
256 devices in a mesh: groups: 2 (over z), ep: 16 (over y, core), rep: 8 (over x).
Axes of the slice: x: 8, y: 8, z: 2, core: 2. Of those that a mesh axis runs over, the one named last changes fastest.
The devices are a block of a 8x8x16 slice.
Arguments:
- prompt_hidden: bfloat16 [8, 384, 2048], P('groups', 'ep'), parts along dimension 0, may hold values from -6 to 6
- decode_hidden: bfloat16 [4096, 8, 2048], P(('groups', 'ep'), 'rep'), parts along dimension 0, may hold values from -6 to 6
- queries: bfloat16 [4096, 8, 2048], P(('groups', 'ep'), None, 'rep'), parts along dimension 0, may hold values from -128 to 128
- attn_gain: float32 [2048], replicated, may hold values from 0.1 to 1.9
- key_value_weight: bfloat16 [2048, 1024], P(None, 'rep'), may hold values from -0.125 to 0.125
- out_weight: bfloat16 [2048, 2048], P('rep'), may hold values from -0.5 to 0.5
- moe_gain: float32 [2048], replicated, may hold values from 0.1 to 1.9
- gate_weight: bfloat16 [128, 2048, 768], P(('ep', 'rep')), may hold values from -0.125 to 0.125
- up_weight: bfloat16 [128, 2048, 768], P(('ep', 'rep')), may hold values from -0.125 to 0.125
- down_weight: bfloat16 [128, 768, 2048], P(('ep', 'rep')), may hold values from -0.21875 to 0.21875
- expert_table: int32 [151936], replicated, may hold values from 0 to 127, as said below
- token_ids: int32 [2048, 8], P('ep', 'rep'), may hold values from 0 to 151935, as said below
- prompt_lengths: int32 [8], P('groups'), parts along dimension 0, may hold values from 1 to 384, 960 in all
Outputs:
- layer_out: bfloat16 [4096, 8, 2048], P(('groups', 'ep'), 'rep'), parts along dimension 0
There are 2 independent parts, one for each index of `groups`. A program takes and returns all parts, laid end to end along the dimension named above; an argument that names none is the same for every part. Nothing has to cross between parts.
Inputs may be any that keep to these rules, and one draw needn't show every extreme that they name: `expert_table`: each expert is the value of exactly 1187 entries. `token_ids`: a device holds the 128 sequences of its index of ep at 8 // 8 steps of its index of rep; of these tokens at most 2 go to one expert; in every draw one expert receives exactly 2 from every device. `prompt_lengths`: the lengths of a group sum to 960 and the longest is 384.
All inputs are finite; a program needn't handle non-finite values.
Results may differ from a plain program's by a relative error of at most 0.017.
The roundings to bfloat16 on the way count: a program that leaves them out, or rounds other values in their place, can miss the bound.
Values may be sent and summed in bfloat16 or wider, within the bound.
A program may use at most 128 MiB of HBM per device.

v0:
```python
import math

import jax
import jax.numpy as jnp
from jax import lax
from jax.sharding import PartitionSpec as P

HEAD_DIM = 128
QUERY_HEADS = 16
KEY_VALUE_HEADS = 4
GROUP_PROMPTS = 4
CAP = 2


EPS = 1e-06
THETA = 1000000.0


def in_one_piece(arrays, axis, dim, along):
    both = jnp.concatenate(arrays, axis=along)
    filled, at, outs = (lax.all_gather(both, axis, axis=dim, tiled=True), 0, [])
    for a in arrays:
        outs.append(lax.slice_in_dim(filled, at, at + a.shape[along], axis=along))
        at += a.shape[along]
    return tuple(outs)


def swapped(block, axis, bit):
    count = lax.axis_size(axis)
    route = []
    for low in range(count):
        high = low | 1 << bit
        if high != low and high < count:
            route += [(low, high), (high, low)]
    return lax.ppermute(block, axis, route)


def rms_scale(hidden, gain_vec):
    widened = hidden.astype(jnp.float32)
    mean_sq = jnp.mean(widened * widened, axis=-1, keepdims=True)
    return widened * lax.rsqrt(mean_sq + EPS) * gain_vec


def rotate(vectors, positions):
    half_dim = vectors.shape[-1] // 2
    inverse_freq = jnp.exp(
        jnp.arange(half_dim, dtype=jnp.float32) * (-2.0 * math.log(THETA) / vectors.shape[-1])
    )
    angles = positions[..., None] * inverse_freq
    cosine = jnp.cos(angles)
    sine_part = jnp.sin(angles)
    first_half = vectors[..., :half_dim]
    second_half = vectors[..., half_dim:]
    return jnp.concatenate(
        [
            first_half * cosine - second_half * sine_part,
            second_half * cosine + first_half * sine_part,
        ],
        axis=-1,
    )


def expert_apply(tokens, gate_weight, up_weight, down_weight):
    flat_rows = tokens.reshape(-1, tokens.shape[-1])
    gate_proj = jnp.dot(flat_rows, gate_weight[0], preferred_element_type=jnp.float32)
    up_proj = jnp.dot(flat_rows, up_weight[0], preferred_element_type=jnp.float32)
    hidden = (jax.nn.silu(gate_proj) * up_proj).astype(jnp.bfloat16)
    return (
        jnp.dot(hidden, down_weight[0], preferred_element_type=jnp.float32)
        .astype(jnp.bfloat16)
        .reshape(tokens.shape)
    )


def local(
    prompt_hidden,
    decode_hidden,
    queries,
    attn_gain,
    key_value_weight,
    out_weight,
    moe_gain,
    gate_weight,
    up_weight,
    down_weight,
    expert_table,
    token_ids,
    prompt_lengths,
):
    full_hidden = lax.all_gather(decode_hidden, "rep", axis=1, tiled=True)
    sequences_local, steps_total, model_width = full_hidden.shape
    prompt_length_local = prompt_hidden.shape[1]
    qh_dev = queries.shape[2] // HEAD_DIM
    group_count = QUERY_HEADS // KEY_VALUE_HEADS
    ep_count = lax.axis_size("ep")
    rep_count = lax.axis_size("rep")
    ep_index = lax.axis_index("ep")
    rep_index = lax.axis_index("rep")
    seq_total = sequences_local * ep_count
    samples = seq_total // GROUP_PROMPTS
    score_scale = HEAD_DIM ** (-0.5)
    step_rows = steps_total // rep_count
    blocks = key_value_weight.shape[1] // HEAD_DIM

    def own_columns(hidden, positions):
        leading = hidden.shape[:-1]
        normed = rms_scale(hidden, attn_gain).astype(jnp.bfloat16)
        projected = jnp.dot(
            normed.reshape(-1, model_width), key_value_weight, preferred_element_type=jnp.float32
        )
        projected = projected.reshape(leading + (blocks, HEAD_DIM))
        block_ids = rep_index * blocks + jnp.arange(blocks, dtype=jnp.int32)
        is_key = (block_ids % 2 == 0)[:, None]
        turned = rotate(projected, positions[..., None])
        return (
            jnp.where(is_key, turned, projected)
            .astype(jnp.bfloat16)
            .reshape(leading + (blocks * HEAD_DIM,))
        )

    key_pos = ep_index * prompt_length_local + jnp.arange(prompt_length_local, dtype=jnp.int32)
    prompt_pos = jnp.broadcast_to(
        key_pos.astype(jnp.float32)[None, :], (GROUP_PROMPTS, prompt_length_local)
    )
    own_seqs = ep_index * sequences_local + jnp.arange(sequences_local, dtype=jnp.int32)
    own_prompt = own_seqs // samples
    own_lengths = jnp.take(prompt_lengths, own_prompt)
    decode_pos = (
        own_lengths[:, None].astype(jnp.float32)
        + jnp.arange(steps_total, dtype=jnp.float32)[None, :]
    )
    prompt_part = own_columns(prompt_hidden, prompt_pos)
    decode_part = own_columns(full_hidden, decode_pos)
    prompt_hot = own_prompt[:, None] == jnp.arange(GROUP_PROMPTS, dtype=jnp.int32)[None, :]
    partner_prompt, partner_decode = swapped((prompt_part, decode_part), "rep", 0)
    holds_key = rep_index % 2 == 0
    prompt_columns = jnp.where(
        holds_key,
        jnp.concatenate([prompt_part, partner_prompt], axis=2),
        jnp.concatenate([partner_prompt, prompt_part], axis=2),
    )
    decode_columns = jnp.where(
        holds_key,
        jnp.concatenate([decode_part, partner_decode], axis=2),
        jnp.concatenate([partner_decode, decode_part], axis=2),
    )
    heads_here = 1
    head_base = rep_index // 2
    prompt_key_value = prompt_columns.reshape(
        GROUP_PROMPTS, prompt_length_local, heads_here, 2, HEAD_DIM
    )
    decode_key_value = decode_columns.reshape(sequences_local, steps_total, heads_here, 2, HEAD_DIM)
    prompt_keys = prompt_key_value[:, :, :, 0, :]
    prompt_values = prompt_key_value[:, :, :, 1, :]
    decode_keys = decode_key_value[:, :, :, 0, :]
    decode_values = decode_key_value[:, :, :, 1, :]
    query_matrix = queries.reshape(sequences_local, steps_total, qh_dev, HEAD_DIM)
    head_pick = (
        rep_index * qh_dev + jnp.arange(qh_dev, dtype=jnp.int32)
    ) // group_count - head_base
    own_keys = jnp.take(decode_keys, head_pick, axis=2)
    own_values = jnp.take(decode_values, head_pick, axis=2)
    self_scores = (
        jnp.einsum("sthd,suhd->sthu", query_matrix, own_keys, preferred_element_type=jnp.float32)
        * score_scale
    )
    self_mask = (
        jnp.arange(steps_total, dtype=jnp.int32)[None, :]
        <= jnp.arange(steps_total, dtype=jnp.int32)[:, None]
    )[None, :, None, :]
    self_scores = jnp.where(self_mask, self_scores, -1e30)
    self_top = jnp.max(self_scores, axis=-1)
    start_weights = jnp.where(self_mask, jnp.exp(self_scores - self_top[..., None]), 0.0)
    pieces = in_one_piece((prompt_keys, prompt_values), "ep", 1, 0)
    row_top = self_top
    row_total = jnp.sum(start_weights, axis=-1)
    weighted = jnp.einsum(
        "sthu,suhd->sthd",
        start_weights.astype(jnp.bfloat16),
        own_values,
        preferred_element_type=jnp.float32,
    )
    piece_keys = jnp.take(pieces[0], head_pick, axis=2)
    piece_values = jnp.take(pieces[1], head_pick, axis=2)
    piece_len = piece_keys.shape[1]
    valid = jnp.arange(piece_len, dtype=jnp.int32)[None, :] < prompt_lengths[:, None]
    key_mask = prompt_hot[:, None, None, :, None] & valid[None, None, None, :, :]
    scores = (
        jnp.einsum("sthd,pnhd->sthpn", query_matrix, piece_keys, preferred_element_type=jnp.float32)
        * score_scale
    )
    scores = jnp.where(key_mask, scores, -1e30)
    new_top = jnp.maximum(row_top, jnp.max(scores, axis=(-2, -1)))
    decay = jnp.exp(row_top - new_top)
    weights = jnp.where(key_mask, jnp.exp(scores - new_top[..., None, None]), 0.0)
    weighted = weighted * decay[..., None] + jnp.einsum(
        "sthpn,pnhd->sthd",
        weights.astype(jnp.bfloat16),
        piece_values,
        preferred_element_type=jnp.float32,
    )
    row_top, row_total, weighted = (
        new_top,
        row_total * decay + jnp.sum(weights, axis=(-2, -1)),
        weighted,
    )
    attended = weighted / row_total[..., None]
    heads_out = attended.reshape(sequences_local, steps_total, qh_dev * HEAD_DIM).astype(
        jnp.bfloat16
    )
    by_step = jnp.swapaxes(heads_out, 0, 1)
    attn_sum = jnp.swapaxes(
        lax.psum_scatter(
            jnp.dot(
                by_step.reshape(-1, by_step.shape[-1]),
                out_weight,
                preferred_element_type=jnp.float32,
            )
            .reshape(step_rows * lax.axis_size("rep"), sequences_local, model_width)
            .astype(jnp.bfloat16),
            "rep",
            scatter_dimension=0,
            tiled=True,
        ).astype(jnp.float32),
        0,
        1,
    )
    attn_mixed = (decode_hidden.astype(jnp.float32) + attn_sum).astype(jnp.bfloat16)
    row_count = sequences_local * step_rows
    normed = rms_scale(attn_mixed, moe_gain).astype(jnp.bfloat16).reshape(row_count, model_width)
    chosen = jnp.take(expert_table, token_ids.reshape(row_count))
    device_count = ep_count * rep_count
    slot_total = device_count * CAP
    same_expert = chosen[:, None] == chosen[None, :]
    before = jnp.arange(row_count)[None, :] < jnp.arange(row_count)[:, None]
    slot_rank = jnp.sum((same_expert & before).astype(jnp.int32), axis=1)
    destination = chosen * CAP + slot_rank
    send_pick = (jnp.arange(slot_total, dtype=jnp.int32)[:, None] == destination[None, :]).astype(
        jnp.bfloat16
    )
    outgoing = (
        jnp.dot(send_pick, normed, preferred_element_type=jnp.float32)
        .astype(jnp.bfloat16)
        .reshape(device_count, CAP, model_width)
    )
    served = expert_apply(
        lax.all_to_all(outgoing, ("ep", "rep"), split_axis=0, concat_axis=0, tiled=True),
        gate_weight,
        up_weight,
        down_weight,
    )
    returned = lax.all_to_all(served, ("ep", "rep"), split_axis=0, concat_axis=0, tiled=True)
    moe_out = lax.dot_general(
        send_pick,
        returned.reshape(slot_total, model_width),
        (((0,), (0,)), ((), ())),
        preferred_element_type=jnp.float32,
    )
    layer_out = (
        attn_mixed.astype(jnp.float32) + moe_out.reshape(sequences_local, step_rows, model_width)
    ).astype(jnp.bfloat16)
    return layer_out


def solution(mesh):
    placed = (
        P("groups", "ep", None),
        P(("groups", "ep"), "rep", None),
        P(("groups", "ep"), None, "rep"),
        P(),
        P(None, "rep"),
        P("rep", None),
        P(),
        P(("ep", "rep"), None, None),
        P(("ep", "rep"), None, None),
        P(("ep", "rep"), None, None),
        P(),
        P("ep", "rep"),
        P("groups"),
    )
    return jax.shard_map(
        local,
        mesh=mesh,
        in_specs=placed,
        out_specs=P(("groups", "ep"), "rep", None),
        check_vma=False,
    )
```

profile of v0, /device:TPU:513, one launch (start us, length us, event | category | flops | bytes accessed | tf_op | source)
XLA Modules:
  0.0 316.9 jit_solution(7113456730417869289)
XLA Ops:
  6.6 0.7 all-gather.2.cloned.1.call-update
  7.3 0.1 reduce-scatter.2.cloned.1.call-start
  7.4 1.2 fusion.39
  8.7 1.2 fusion.41
  9.8 1.3 fusion.110
  11.2 0.1 fusion.91
  11.3 0.1 fusion.94
  11.4 2.3 collective-permute-start.1
  13.7 1.5 fusion.109
  15.1 2.5 fusion.100
  17.7 0.5 iota_compare_fusion.5
  18.2 0.7 iota_compare_fusion.4
  18.9 0.7 iota_add_fusion
  19.6 0.9 broadcast_and_fusion
  20.6 0.5 compare_and_fusion
  21.2 0.1 fusion.108
  21.3 35.0 %all_gather.7 = bf16[8,384,1,128]{3,0,2,1:T(8,128)(2,1)S(1)} all-gather(bf16[8,24,1,128]{3,0,2,1:T(8,128)(2,1)S(1)} %copy.139), channel_id=1, replica_groups=mesh['groups'=2,'ep'=16,'rep'=8] {'ep'}, dimensions={1}, use_global_device_ids=true | all-gather | bytes 835584 | tf_op jit(solution)/shard_map/all_gather | solution.py:21
  56.3 0.3 slice_bitcast_fusion
  56.6 0.8 copy.140
  57.3 26.0 %all-gather.2.cloned.1.call-done = bf16[128,8,2048]{2,0,1:T(8,128)(2,1)} async-done(((bf16[128,1,2048]{2,0,1:T(8,128)(2,1)}), bf16[128,8,2048]{2,0,1:T(8,128)(2,1)}) %all-gather.2.cloned.1.call-update) | async-done | bytes 4194320 | tf_op jit(solution)/shard_map/all_gather | solution.py:90
  83.4 5.1 %fusion.3 = f32[128,8]{1,0:T(8,128)} fusion(bf16[128,8,2048]{2,0,1:T(8,128)(2,1)} %all-gather.2.cloned.1.call-done), kind=kLoop, calls=%fused_computation.8 | loop fusion | flops 6290432 | bytes 4198400 | tf_op jit(solution)/shard_map/reduce_sum | solution.py:40
  88.5 0.9 copy.131
  89.4 0.7 copy.132
  90.2 0.0 copy-start.6
  90.2 5.0 %fusion.7 = f32[1024,128]{1,0:T(8,128)S(1)} fusion(bf16[2048,128]{1,0:T(8,128)(2,1)} %param.21, f32[2048]{0:T(1024)S(1)} %copy-done.10, f32[128,8]{1,0:T(8,128)} %copy.132, bf16[128,8,2048]{2,0,1:T(8,128)(2,1)} %all-gather.2.cloned.1.call-done), kind=kOutput, calls=%fused_computation.12 | convolution fusion | flops 545259520 | bytes 5255168 | tf_op jit(solution)/shard_map/dot_general | solution.py:108
  95.2 2.4 fusion.56
  97.6 0.2 fusion.61
  97.8 0.3 collective-permute-start
  98.1 5.7 %fusion = (f32[128,8,2]{0,1,2:T(8,128)S(1)}, f32[2,4,384,128,8]{3,2,4,1,0:T(8,128)}) fusion(pred[128,4,384]{0,2,1:T(8,128)(4,1)S(1)} %copy-done.3, bf16[128,8,2,128,1]{3,1,2,0,4:T(8,128)(2,1)S(1)} %bitcast.168, pred[2]{0:T(512)(128)(4,1)S(1)} %copy-done.14, bf16[4,384,128]{2,1,0:T(8,128)(2,1)S(1)} %copy-done.6), kind=kOutput, calls=%fused_computation.3 | convolution fusion | flops 815134720 | bytes 13705218 | tf_op jit(solution)/shard_map/sthd,pnhd->sthpn/dot_general | solution.py:189
  103.8 0.8 copy.145
  104.6 0.5 collective-permute-done
  105.1 0.2 fusion.62
  105.3 0.8 slice_bitcast_fusion.3
  106.0 1.5 fusion.64
  107.5 1.6 copy.135
  109.2 0.7 fusion.89
  109.9 1.9 fusion.95
  111.8 9.7 %fusion.2 = (bf16[128,8,2,4,384]{0,4,1,3,2:T(8,128)(2,1)}, f32[128,8,2]{0,1,2:T(8,128)S(1)}) fusion(f32[2,4,384,128,8]{3,2,4,1,0:T(8,128)} %get-tuple-element.28, f32[128,8,2]{0,1,2:T(8,128)S(1)} %copy_maximum_fusion, pred[128,4,384]{0,2,1:T(8,128)(4,1)} %broadcast_and_fusion), kind=kLoop, calls=%fused_computation.7 | loop fusion | flops 18872320 | bytes 19087360 | tf_op jit(solution)/shard_map/convert_element_type | solution.py:198
  121.5 9.0 %copy.146 = bf16[128,8,2,4,384]{4,1,3,2,0:T(8,128)(2,1)} copy(bf16[128,8,2,4,384]{0,4,1,3,2:T(8,128)(2,1)} %get-tuple-element.9) | data formatting | bytes 12582912 | tf_op jit(solution)/shard_map/convert_element_type | solution.py:198
  130.6 1.4 fusion.97
  131.9 1.5 copy.144
  133.4 1.9 copy.138
  135.4 1.5 copy.149
  136.8 1.8 fusion.25
  138.7 1.2 copy-done.1
  139.9 2.6 fusion.33
  142.6 0.0 copy-start.15
  142.6 0.0 copy-start.11
  142.6 3.2 %convolution_convert_fusion = bf16[8,128,2048]{2,1,0:T(8,128)(2,1)} fusion(bf16[256,2048]{1,0:T(8,128)(2,1)S(1)} %copy-done.2, bf16[8,128,256]{2,0,1:T(8,128)(2,1)S(1)} %fusion.33), kind=kOutput, calls=%fused_computation.15 | convolution fusion | flops 1075838976 | bytes 5767168 | tf_op jit(solution)/shard_map/dot_general | solution.py:214
  145.8 0.1 reduce-scatter.2.cloned.1.call-update
  145.9 2.1 gather_fusion
  148.0 0.2 convert_reduce_fusion
  148.2 54.3 %reduce-scatter.2.cloned.1.call-done = bf16[1,128,2048]{2,1,0:T(8,128)(2,1)} async-done(((bf16[8,128,2048]{2,1,0:T(8,128)(2,1)}), bf16[1,128,2048]{2,1,0:T(8,128)(2,1)}) %reduce-scatter.2.cloned.1.call-update) | async-done | bytes 524304 | tf_op jit(solution)/shard_map/reduce_scatter | solution.py:213
  202.5 1.5 fusion.34
  203.9 2.7 convolution_convert_fusion.1
  206.7 2.5 reshape.407
  209.2 42.8 %all_to_all.10 = bf16[128,2,2048]{2,1,0:T(2,128)(2,1)} all-to-all(bf16[128,2,2048]{2,1,0:T(2,128)(2,1)} %reshape.407), channel_id=1, replica_groups=mesh['groups'=2,'ep'=16,'rep'=8] {'ep','rep'}, dimensions={0} | all-to-all | bytes 2097152 | tf_op jit(solution)/shard_map/all_to_all | solution.py:247
  252.0 2.2 reshape.408
  254.3 4.1 %fusion.16 = f32[256,768]{1,0:T(8,128)} fusion(bf16[256,2048]{1,0:T(8,128)(2,1)} %reshape.408, bf16[1,2048,768]{2,1,0:T(8,128)(2,1)} %param.24), kind=kOutput, calls=%fused_computation.21 | convolution fusion | flops 805306368 | bytes 4980736 | tf_op jit(solution)/shard_map/dot_general | solution.py:65
  258.3 5.5 %fusion.18 = bf16[256,2048]{1,0:T(8,128)(2,1)} fusion(bf16[1,768,2048]{2,1,0:T(8,128)(2,1)S(1)} %copy-done, bf16[256,2048]{1,0:T(8,128)(2,1)} %reshape.408, bf16[1,2048,768]{2,1,0:T(8,128)(2,1)} %param.25, f32[256,768]{1,0:T(8,128)} %fusion.16), kind=kOutput, calls=%fused_computation.24 | convolution fusion | flops 1612316672 | bytes 9175040 | tf_op jit(solution)/shard_map/dot_general | solution.py:69
  263.9 2.5 reshape.409
  266.4 38.7 %all_to_all.11 = bf16[128,2,2048]{2,1,0:T(2,128)(2,1)} all-to-all(bf16[128,2,2048]{2,1,0:T(2,128)(2,1)} %reshape.409), channel_id=1, replica_groups=mesh['groups'=2,'ep'=16,'rep'=8] {'ep','rep'}, dimensions={0} | all-to-all | bytes 2097152 | tf_op jit(solution)/shard_map/all_to_all | solution.py:252
  305.1 2.2 reshape.410
  307.3 2.7 fusion.22
  (48 shorter events, 0.2 us)
Async XLA Ops:
  6.5 251.8 %copy-start = (bf16[1,768,2048]{2,1,0:T(8,128)(2,1)S(1)}, bf16[1,768,2048]{2,1,0:T(8,128)(2,1)}, u32[]{:S(2)}) copy-start(bf16[1,768,2048]{2,1,0:T(8,128)(2,1)} %param.26) | copy-start | bytes 9437188
  6.6 83.6 %copy-start.10 = (f32[2048]{0:T(1024)S(1)}, f32[2048]{0:T(1024)}, u32[]{:S(2)}) copy-start(f32[2048]{0:T(1024)} %param.20) | copy-start | bytes 24580
  6.6 76.8 %all-gather.2.cloned.1.call-start = ((), (), s32[]{:S(2)}) async-start(), calls=%async_computation.3 | async-start | bytes 4718592 | tf_op jit(solution)/shard_map/all_gather | solution.py:90
  7.3 195.2 %reduce-scatter.2.cloned.1.call-start = ((), (), s32[]{:S(2)}) async-start(), calls=%async_computation.4 | async-start | bytes 4718592 | tf_op jit(solution)/shard_map/reduce_scatter | solution.py:213
  7.4 4.0 %copy-start.12 = (f32[64]{0:T(128)}, f32[64]{0:T(128)S(1)}, u32[]{:S(2)}) copy-start(f32[64]{0:T(128)S(1)} %multiply_exponential_fusion) | copy-start | bytes 772
  11.4 9.7 %collective-permute-start.1 = (bf16[4,24,128]{2,1,0:T(8,128)(2,1)S(1)}, bf16[4,24,128]{2,1,0:T(8,128)(2,1)S(1)}, u32[]{:S(2)}, u32[]{:S(2)}) collective-permute-start(bf16[4,24,128]{2,1,0:T(8,128)(2,1)S(1)} %fusion.94), channel_id=1, source_target_pairs={{0,1},{1,0},{2,3},{3,2},{4,5},{5,4},{6,7},{7,6},{8,9},{9,8},{10,11... | collective-permute-start | bytes 73736 | tf_op jit(solution)/shard_map/ppermute | solution.py:35
  90.2 5.0 %copy-start.7 = (f32[128,8]{1,0:T(8,128)S(1)}, f32[128,8]{1,0:T(8,128)}, u32[]{:S(2)}) copy-start(f32[128,8]{1,0:T(8,128)} %iota_add_fusion) | copy-start | bytes 12292
  90.2 5.0 %copy-start.13 = (f32[64]{0:T(128)S(1)}, f32[64]{0:T(128)}, u32[]{:S(2)}) copy-start(f32[64]{0:T(128)} %copy-done.12) | copy-start | bytes 772
  90.2 7.9 %copy-start.3 = (pred[128,4,384]{0,2,1:T(8,128)(4,1)S(1)}, pred[128,4,384]{0,2,1:T(8,128)(4,1)}, u32[]{:S(2)}) copy-start(pred[128,4,384]{0,2,1:T(8,128)(4,1)} %broadcast_and_fusion) | copy-start | bytes 589828
  90.2 7.9 %copy-start.4 = (bf16[128,8,256]{2,1,0:T(8,128)(2,1)S(1)}, bf16[128,8,256]{2,1,0:T(8,128)(2,1)}, u32[]{:S(2)}) copy-start(bf16[128,8,256]{2,1,0:T(8,128)(2,1)} %param.19) | copy-start | bytes 1572868
  90.2 7.9 %copy-start.6 = (bf16[4,384,128]{2,1,0:T(8,128)(2,1)S(1)}, bf16[4,384,128]{2,1,0:T(8,128)(2,1)}, u32[]{:S(2)}) copy-start(bf16[4,384,128]{2,1,0:T(8,128)(2,1)} %copy.140) | copy-start | bytes 1179652
  90.2 7.9 %copy-start.14 = (pred[2]{0:T(512)(128)(4,1)S(1)}, pred[2]{0:T(512)(128)(4,1)}, u32[]{:S(2)}) copy-start(pred[2]{0:T(512)(128)(4,1)} %compare_and_fusion) | copy-start | bytes 10
  97.8 7.3 %collective-permute-start = (bf16[128,8,128]{2,1,0:T(8,128)(2,1)S(1)}, bf16[128,8,128]{2,1,0:T(8,128)(2,1)S(1)}, u32[]{:S(2)}, u32[]{:S(2)}) collective-permute-start(bf16[128,8,128]{2,1,0:T(8,128)(2,1)S(1)} %fusion.61), channel_id=1, source_target_pairs={{0,1},{1,0},{2,3},{3,2},{4,5},{5,4},{6,7},{7,6},{8,9},{9,8},{10,11... | collective-permute-start | bytes 786440 | tf_op jit(solution)/shard_map/ppermute | solution.py:35
  103.8 8.0 %copy-start.9 = (f32[128,8,2]{0,1,2:T(8,128)}, f32[128,8,2]{0,1,2:T(8,128)S(1)}, u32[]{:S(2)}) copy-start(f32[128,8,2]{0,1,2:T(8,128)S(1)} %get-tuple-element.27) | copy-start | bytes 24580
  130.6 8.1 %copy-start.5 = (bf16[4,384,128]{2,1,0:T(8,128)(2,1)S(1)}, bf16[4,384,128]{2,1,0:T(8,128)(2,1)}, u32[]{:S(2)}) copy-start(bf16[4,384,128]{2,1,0:T(8,128)(2,1)} %copy.145) | copy-start | bytes 1179652
  136.8 3.1 copy-start.1
  136.8 3.1 copy-start.8
  139.9 2.6 copy-start.2
  142.6 3.3 %copy-start.15 = (s32[128,1]{0,1:T(1,128)S(1)}, s32[128,1]{0,1:T(1,128)}, u32[]{:S(2)}) copy-start(s32[128,1]{0,1:T(1,128)} %param.28) | copy-start | bytes 1540
  142.6 61.4 %copy-start.11 = (f32[2048]{0:T(1024)S(1)}, f32[2048]{0:T(1024)}, u32[]{:S(2)}) copy-start(f32[2048]{0:T(1024)} %param.23) | copy-start | bytes 24580
Sparse Core Ops, SparseCore 0:
  9.1 74.2 all-gather.1
  146.0 56.4 reduce-scatter.1
where the time goes:
time: 318 us; the launch traced here: 317 us
  blocking collectives  116 us (36%)
  waiting for transfers between devices  81.6 us (26%)
  matrix products  36.1 us (11%)
  local copies, waits for them, and re-layouts  34.3 us (11%)
  other arithmetic  31.9 us (10%)
  between operations  13.8 us (4%)
    reduce_scatter x1, waiting for transfers between devices, local(): lax.psum_scatter(jnp.dot(by_step.reshape(-1, by_step.shape[-1]), out_weig...  54.3 us
    all_to_all x1, blocking collectives, local(): lax.all_to_all(outgoing, ('ep', 'rep'), split_axis=0, concat_axis=0, tile...  42.8 us
    all_to_all x1, blocking collectives, local(): lax.all_to_all(served, ('ep', 'rep'), split_axis=0, concat_axis=0, tiled=...  38.7 us
    all_gather x1, blocking collectives, in_one_piece(): filled, at, outs = (lax.all_gather(both, axis, axis=dim, tiled=True), 0, [])  35 us
    all_gather x1, waiting for transfers between devices, local(): full_hidden = lax.all_gather(decode_hidden, 'rep', axis=1, tiled=True)  26 us
    convert_element_type x1, other arithmetic, local(): weights.astype(jnp.bfloat16)  9.72 us
    convert_element_type x1, local copies, waits for them, and re-layouts, local(): weights.astype(jnp.bfloat16)  9.02 us
    reduce_sum x3, other arithmetic, rms_scale(): mean_sq = jnp.mean(widened * widened, axis=-1, keepdims=True)  7.81 us
  transfers between devices with their start and end apart: 4, of which 3 were waited for; matrix products, arithmetic and copies ran while one was open for 7% of the time, Pallas kernels for 0%

commit v1 on v0

--- a/solution.py
+++ b/solution.py
@@ -1,8 +1,11 @@
+import functools
 import math
 
 import jax
 import jax.numpy as jnp
 from jax import lax
+from jax.experimental import pallas as pl
+from jax.experimental.pallas import tpu as pltpu
 from jax.sharding import PartitionSpec as P
 
 HEAD_DIM = 128
@@ -11,9 +14,11 @@
 GROUP_PROMPTS = 4
 CAP = 2
 
-
 EPS = 1e-06
 THETA = 1000000.0
+MESH = pl.DeviceIdType.MESH
+F32 = jnp.float32
+BF16 = jnp.bfloat16
 
 
 def in_one_piece(arrays, axis, dim, along):
@@ -36,7 +41,7 @@
 
 
 def rms_scale(hidden, gain_vec):
-    widened = hidden.astype(jnp.float32)
+    widened = hidden.astype(F32)
     mean_sq = jnp.mean(widened * widened, axis=-1, keepdims=True)
     return widened * lax.rsqrt(mean_sq + EPS) * gain_vec
 
@@ -44,7 +49,7 @@
 def rotate(vectors, positions):
     half_dim = vectors.shape[-1] // 2
     inverse_freq = jnp.exp(
-        jnp.arange(half_dim, dtype=jnp.float32) * (-2.0 * math.log(THETA) / vectors.shape[-1])
+        jnp.arange(half_dim, dtype=F32) * (-2.0 * math.log(THETA) / vectors.shape[-1])
     )
     angles = positions[..., None] * inverse_freq
     cosine = jnp.cos(angles)
@@ -60,15 +65,191 @@
     )
 
 
-def expert_apply(tokens, gate_weight, up_weight, down_weight):
-    flat_rows = tokens.reshape(-1, tokens.shape[-1])
-    gate_proj = jnp.dot(flat_rows, gate_weight[0], preferred_element_type=jnp.float32)
-    up_proj = jnp.dot(flat_rows, up_weight[0], preferred_element_type=jnp.float32)
-    hidden = (jax.nn.silu(gate_proj) * up_proj).astype(jnp.bfloat16)
-    return (
-        jnp.dot(hidden, down_weight[0], preferred_element_type=jnp.float32)
-        .astype(jnp.bfloat16)
-        .reshape(tokens.shape)
+def dot(a, b):
+    return jnp.dot(a, b, preferred_element_type=F32)
+
+
+def dot_t(a, b):
+    return lax.dot_general(a, b, (((0,), (0,)), ((), ())), preferred_element_type=F32)
+
+
+def one_hot(hit):
+    return jnp.where(hit, 1.0, 0.0).astype(BF16)
+
+
+def moe_kernel(
+    nx, ne, mixed_ref, gain_ref, row_ref, col_ref, gate_hbm, up_hbm, down_hbm, out_ref,
+    gate, up, down, normed, xin, hid,
+    s0, s1, r0, r1, t0, t1, q0, q1, o0, o1, b0, b1, c0, c1, f0, f1,
+    wsem, ssem, rsem,
+):
+    e, x, g = lax.axis_index("ep"), lax.axis_index("rep"), lax.axis_index("groups")
+    rows, width = mixed_ref.shape
+    ff = gate.shape[1]
+    half = nx * ne
+    loads = [
+        pltpu.make_async_copy(gate_hbm, gate, wsem.at[0]),
+        pltpu.make_async_copy(up_hbm, up, wsem.at[1]),
+        pltpu.make_async_copy(down_hbm, down, wsem.at[2]),
+    ]
+    for load in loads:
+        load.start()
+    barrier = pltpu.get_barrier_semaphore()
+    for i in range(1, nx):
+        peer = (g, e, lax.rem(x + i, nx))
+        pl.semaphore_signal(barrier, inc=1, device_id=peer, device_id_type=MESH)
+    for i in range(1, ne):
+        peer = (g, lax.rem(e + i, ne), x)
+        pl.semaphore_signal(barrier, inc=1, device_id=peer, device_id_type=MESH)
+
+    widened = mixed_ref[...].astype(F32)
+    scale = lax.rsqrt(jnp.mean(widened * widened, axis=-1, keepdims=True) + EPS)
+    normed[...] = (widened * scale * gain_ref[...]).astype(BF16)
+
+    row, col = row_ref[...], col_ref[...]
+    first = lax.broadcasted_iota(jnp.int32, (rows, rows), 0)
+    second = lax.broadcasted_iota(jnp.int32, (rows, rows), 1)
+    earlier = jnp.where((row == col) & (first < second), 1, 0)
+    rank = jnp.sum(earlier, axis=0, keepdims=True)
+    slot = lax.broadcasted_iota(jnp.int32, (half, rows), 0)
+    turned = lax.rem(slot, ne) * nx + slot // ne
+    pick0 = one_hot((turned == row) & (rank == 0))
+    pick1 = one_hot((slot == row) & (rank == 1))
+
+    here = lax.broadcasted_iota(jnp.int32, (half, half), 0)
+    there = lax.broadcasted_iota(jnp.int32, (half, half), 1)
+    to_ex = one_hot(there == lax.rem(here, nx) * ne + here // nx)
+    to_xe = one_hot(there == lax.rem(here, ne) * nx + here // ne)
+
+    tile = 512
+
+    def over_columns(body):
+        def step(i, carry):
+            body(pl.ds(pl.multiple_of(i * tile, tile), tile))
+            return carry
+
+        lax.fori_loop(0, width // tile, step, 0)
+
+    def put(ref, cols, value):
+        ref[:, :, cols] = value.reshape(ref.shape[0], ref.shape[1], tile).astype(BF16)
+
+    def get(ref, cols):
+        return ref[:, :, cols].astype(F32).reshape(half, tile).astype(BF16)
+
+    def send_x(src, dst, k):
+        for i in range(1, nx):
+            to = lax.rem(x + i, nx)
+            pltpu.make_async_remote_copy(
+                src.at[to], dst.at[x], ssem.at[k], rsem.at[k],
+                device_id=(g, e, to), device_id_type=MESH,
+            ).start()
+
+    def send_e(src, dst, k):
+        for i in range(1, ne):
+            to = lax.rem(e + i, ne)
+            pltpu.make_async_remote_copy(
+                src.at[to], dst.at[e], ssem.at[k], rsem.at[k],
+                device_id=(g, to, x), device_id_type=MESH,
+            ).start()
+
+    def arrive(src, dst, k):
+        n = dst.shape[0] - 1
+        pltpu.make_async_copy(src.at[pl.ds(0, n)], dst.at[pl.ds(0, n)], ssem.at[k]).wait()
+        pltpu.make_async_copy(src.at[pl.ds(0, n)], dst.at[pl.ds(0, n)], rsem.at[k]).wait()
+
+    def scatter(cols):
+        put(s0, cols, dot(pick0, normed[:, cols]))
+        put(s1, cols, dot(pick1, normed[:, cols]))
+
+    over_columns(scatter)
+    pl.semaphore_wait(barrier, nx + ne - 2)
+    send_x(s0, r0, 0)
+    send_e(s1, r1, 1)
+    r0[x] = s0[x]
+    r1[e] = s1[e]
+    arrive(s0, r0, 0)
+    over_columns(lambda cols: put(t0, cols, dot(to_ex, get(r0, cols))))
+    send_e(t0, q0, 2)
+    q0[e] = t0[e]
+    arrive(s1, r1, 1)
+    over_columns(lambda cols: put(t1, cols, dot(to_xe, get(r1, cols))))
+    send_x(t1, q1, 3)
+    q1[x] = t1[x]
+
+    for load in loads:
+        load.wait()
+    arrive(t0, q0, 2)
+    arrive(t1, q1, 3)
+
+    def collect(cols):
+        xin[pl.ds(0, half), cols] = get(q0, cols)
+        xin[pl.ds(half, half), cols] = get(q1, cols)
+
+    over_columns(collect)
+    ftile = 256
+
+    def inner(i, carry):
+        cols = pl.ds(pl.multiple_of(i * ftile, ftile), ftile)
+        gate_proj = dot(xin[...], gate[:, cols])
+        up_proj = dot(xin[...], up[:, cols])
+        hid[:, cols] = (jax.nn.silu(gate_proj) * up_proj).astype(BF16)
+        return carry
+
+    lax.fori_loop(0, ff // ftile, inner, 0)
+
+    def outer(cols):
+        put(o0, cols, dot(hid[pl.ds(0, half), :], down[:, cols]))
+        put(o1, cols, dot(hid[pl.ds(half, half), :], down[:, cols]))
+
+    over_columns(outer)
+    send_e(o0, b0, 4)
+    send_x(o1, b1, 5)
+    b0[e] = o0[e]
+    b1[x] = o1[x]
+    arrive(o0, b0, 4)
+    over_columns(lambda cols: put(c0, cols, dot(to_xe, get(b0, cols))))
+    send_x(c0, f0, 6)
+    f0[x] = c0[x]
+    arrive(o1, b1, 5)
+    over_columns(lambda cols: put(c1, cols, dot(to_ex, get(b1, cols))))
+    send_e(c1, f1, 7)
+    f1[e] = c1[e]
+    arrive(c0, f0, 6)
+    arrive(c1, f1, 7)
+
+    def combine(cols):
+        moe = dot_t(pick0, get(f0, cols)) + dot_t(pick1, get(f1, cols))
+        out_ref[:, cols] = (mixed_ref[:, cols].astype(F32) + moe).astype(BF16)
+
+    over_columns(combine)
+
+
+def moe(mixed, gain, chosen, gate_weight, up_weight, down_weight):
+    nx, ne = lax.axis_size("rep"), lax.axis_size("ep")
+    rows, width = mixed.shape
+    ff = gate_weight.shape[2]
+    half = nx * ne
+    xe = pltpu.VMEM((nx, ne, width), BF16)
+    ex = pltpu.VMEM((ne, nx, width), BF16)
+    vmem, any_ = pl.BlockSpec(memory_space=pltpu.VMEM), pl.BlockSpec(memory_space=pl.ANY)
+    return pl.pallas_call(
+        functools.partial(moe_kernel, nx, ne),
+        out_shape=jax.ShapeDtypeStruct((rows, width), BF16),
+        in_specs=[vmem] * 4 + [any_] * 3,
+        out_specs=vmem,
+        scratch_shapes=[
+            pltpu.VMEM((width, ff), BF16), pltpu.VMEM((width, ff), BF16), pltpu.VMEM((ff, width), BF16),
+            pltpu.VMEM((rows, width), BF16), pltpu.VMEM((2 * half, width), BF16), pltpu.VMEM((2 * half, ff), BF16),
+            xe, ex, xe, ex, ex, xe, ex, xe, ex, xe, ex, xe, xe, ex, xe, ex,
+            pltpu.SemaphoreType.DMA((3,)), pltpu.SemaphoreType.DMA((8,)), pltpu.SemaphoreType.DMA((8,)),
+        ],
+        compiler_params=pltpu.CompilerParams(
+            collective_id=1, has_side_effects=True, vmem_limit_bytes=48 << 20
+        ),
+        name="moe",
+    )(
+        mixed, gain.reshape(1, width), chosen.reshape(1, rows), chosen.reshape(rows, 1),
+        gate_weight[0], up_weight[0], down_weight[0],
     )
 
 
@@ -104,9 +285,9 @@
 
     def own_columns(hidden, positions):
         leading = hidden.shape[:-1]
-        normed = rms_scale(hidden, attn_gain).astype(jnp.bfloat16)
+        normed = rms_scale(hidden, attn_gain).astype(BF16)
         projected = jnp.dot(
-            normed.reshape(-1, model_width), key_value_weight, preferred_element_type=jnp.float32
+            normed.reshape(-1, model_width), key_value_weight, preferred_element_type=F32
         )
         projected = projected.reshape(leading + (blocks, HEAD_DIM))
         block_ids = rep_index * blocks + jnp.arange(blocks, dtype=jnp.int32)
@@ -114,20 +295,20 @@
         turned = rotate(projected, positions[..., None])
         return (
             jnp.where(is_key, turned, projected)
-            .astype(jnp.bfloat16)
+            .astype(BF16)
             .reshape(leading + (blocks * HEAD_DIM,))
         )
 
     key_pos = ep_index * prompt_length_local + jnp.arange(prompt_length_local, dtype=jnp.int32)
     prompt_pos = jnp.broadcast_to(
-        key_pos.astype(jnp.float32)[None, :], (GROUP_PROMPTS, prompt_length_local)
+        key_pos.astype(F32)[None, :], (GROUP_PROMPTS, prompt_length_local)
     )
     own_seqs = ep_index * sequences_local + jnp.arange(sequences_local, dtype=jnp.int32)
     own_prompt = own_seqs // samples
     own_lengths = jnp.take(prompt_lengths, own_prompt)
     decode_pos = (
-        own_lengths[:, None].astype(jnp.float32)
-        + jnp.arange(steps_total, dtype=jnp.float32)[None, :]
+        own_lengths[:, None].astype(F32)
+        + jnp.arange(steps_total, dtype=F32)[None, :]
     )
     prompt_part = own_columns(prompt_hidden, prompt_pos)
     decode_part = own_columns(full_hidden, decode_pos)
@@ -161,7 +342,7 @@
     own_keys = jnp.take(decode_keys, head_pick, axis=2)
     own_values = jnp.take(decode_values, head_pick, axis=2)
     self_scores = (
-        jnp.einsum("sthd,suhd->sthu", query_matrix, own_keys, preferred_element_type=jnp.float32)
+        jnp.einsum("sthd,suhd->sthu", query_matrix, own_keys, preferred_element_type=F32)
         * score_scale
     )
     self_mask = (
@@ -176,9 +357,9 @@
     row_total = jnp.sum(start_weights, axis=-1)
     weighted = jnp.einsum(
         "sthu,suhd->sthd",
-        start_weights.astype(jnp.bfloat16),
+        start_weights.astype(BF16),
         own_values,
-        preferred_element_type=jnp.float32,
+        preferred_element_type=F32,
     )
     piece_keys = jnp.take(pieces[0], head_pick, axis=2)
     piece_values = jnp.take(pieces[1], head_pick, axis=2)
@@ -186,7 +367,7 @@
     valid = jnp.arange(piece_len, dtype=jnp.int32)[None, :] < prompt_lengths[:, None]
     key_mask = prompt_hot[:, None, None, :, None] & valid[None, None, None, :, :]
     scores = (
-        jnp.einsum("sthd,pnhd->sthpn", query_matrix, piece_keys, preferred_element_type=jnp.float32)
+        jnp.einsum("sthd,pnhd->sthpn", query_matrix, piece_keys, preferred_element_type=F32)
         * score_scale
     )
     scores = jnp.where(key_mask, scores, -1e30)
@@ -195,9 +376,9 @@
     weights = jnp.where(key_mask, jnp.exp(scores - new_top[..., None, None]), 0.0)
     weighted = weighted * decay[..., None] + jnp.einsum(
         "sthpn,pnhd->sthd",
-        weights.astype(jnp.bfloat16),
+        weights.astype(BF16),
         piece_values,
-        preferred_element_type=jnp.float32,
+        preferred_element_type=F32,
     )
     row_top, row_total, weighted = (
         new_top,
@@ -206,7 +387,7 @@
     )
     attended = weighted / row_total[..., None]
     heads_out = attended.reshape(sequences_local, steps_total, qh_dev * HEAD_DIM).astype(
-        jnp.bfloat16
+        BF16
     )
     by_step = jnp.swapaxes(heads_out, 0, 1)
     attn_sum = jnp.swapaxes(
@@ -214,52 +395,24 @@
             jnp.dot(
                 by_step.reshape(-1, by_step.shape[-1]),
                 out_weight,
-                preferred_element_type=jnp.float32,
+                preferred_element_type=F32,
             )
             .reshape(step_rows * lax.axis_size("rep"), sequences_local, model_width)
-            .astype(jnp.bfloat16),
+            .astype(BF16),
             "rep",
             scatter_dimension=0,
             tiled=True,
-        ).astype(jnp.float32),
+        ).astype(F32),
         0,
         1,
     )
-    attn_mixed = (decode_hidden.astype(jnp.float32) + attn_sum).astype(jnp.bfloat16)
+    attn_mixed = (decode_hidden.astype(F32) + attn_sum).astype(BF16)
     row_count = sequences_local * step_rows
-    normed = rms_scale(attn_mixed, moe_gain).astype(jnp.bfloat16).reshape(row_count, model_width)
     chosen = jnp.take(expert_table, token_ids.reshape(row_count))
-    device_count = ep_count * rep_count
-    slot_total = device_count * CAP
-    same_expert = chosen[:, None] == chosen[None, :]
-    before = jnp.arange(row_count)[None, :] < jnp.arange(row_count)[:, None]
-    slot_rank = jnp.sum((same_expert & before).astype(jnp.int32), axis=1)
-    destination = chosen * CAP + slot_rank
-    send_pick = (jnp.arange(slot_total, dtype=jnp.int32)[:, None] == destination[None, :]).astype(
-        jnp.bfloat16
-    )
-    outgoing = (
-        jnp.dot(send_pick, normed, preferred_element_type=jnp.float32)
-        .astype(jnp.bfloat16)
-        .reshape(device_count, CAP, model_width)
-    )
-    served = expert_apply(
-        lax.all_to_all(outgoing, ("ep", "rep"), split_axis=0, concat_axis=0, tiled=True),
-        gate_weight,
-        up_weight,
-        down_weight,
-    )
-    returned = lax.all_to_all(served, ("ep", "rep"), split_axis=0, concat_axis=0, tiled=True)
-    moe_out = lax.dot_general(
-        send_pick,
-        returned.reshape(slot_total, model_width),
-        (((0,), (0,)), ((), ())),
-        preferred_element_type=jnp.float32,
-    )
-    layer_out = (
-        attn_mixed.astype(jnp.float32) + moe_out.reshape(sequences_local, step_rows, model_width)
-    ).astype(jnp.bfloat16)
-    return layer_out
+    out = moe(
+        attn_mixed.reshape(row_count, model_width), moe_gain, chosen, gate_weight, up_weight, down_weight
+    )
+    return out.reshape(sequences_local, step_rows, model_width)
 
 
 def solution(mesh):

time: 318 us -> 272 us (0.86)
  blocking collectives: 116 us -> 35 us
  Pallas kernels: 0 us -> 71.7 us
  local copies, waits for them, and re-layouts: 34.3 us -> 16.7 us
  matrix products: 36.1 us -> 20.7 us
  other arithmetic: 31.9 us -> 24.9 us
  waiting for transfers between devices: 81.6 us -> 85.6 us
    all_to_all x2 -> x0, blocking collectives: 81.5 us -> none  [the longest x1 42.8 us: local(): lax.all_to_all(outgoing, ('ep', 'rep'), split_axis=0, concat_axis=0, tile...]
    pallas_call x0 -> x1, Pallas kernels: none -> 71.7 us  [moe(): pl.pallas_call(functools.partial(moe_kernel, nx, ne), out_shape=jax.Shape...]
    dot_general x6 -> x2, matrix products: 19.5 us -> 5.23 us  [the longest x1 4.69 us: local(): jnp.einsum('sthpn,pnhd->sthd', weights.astype(BF16), piece_values, prefer...]
    reshape x4 -> x0, local copies, waits for them, and re-layouts: 9.56 us -> none  [the longest x1 2.53 us: local(): outgoing = jnp.dot(send_pick, normed, preferred_element_type=jnp.float32)...]
    reduce_sum x3 -> x2, other arithmetic: 7.81 us -> 5.67 us  [rms_scale(): mean_sq = jnp.mean(widened * widened, axis=-1, keepdims=True)]
  transfers between devices with their start and end apart: 4 -> 4, of which waited for: 3 -> 3; matrix products, arithmetic and copies ran while one was open for 7% -> 6% of each run, Pallas kernels for 0% -> 0%
where the time goes in v1:
time: 272 us; the launch traced here: 271 us
  waiting for transfers between devices  85.6 us (31%)
  Pallas kernels  71.7 us (26%)
  blocking collectives  35 us (13%)
  other arithmetic  24.9 us (9%)
  matrix products  20.7 us (8%)
  local copies, waits for them, and re-layouts  16.7 us (6%)
  between operations  13.9 us (5%)
    pallas_call x1, Pallas kernels, moe(): pl.pallas_call(functools.partial(moe_kernel, nx, ne), out_shape=jax.Shape...  71.7 us
    reduce_scatter x1, waiting for transfers between devices, local(): lax.psum_scatter(jnp.dot(by_step.reshape(-1, by_step.shape[-1]), out_weig...  54.6 us
    all_gather x1, blocking collectives, in_one_piece(): filled, at, outs = (lax.all_gather(both, axis, axis=dim, tiled=True), 0, [])  35 us
    all_gather x1, waiting for transfers between devices, local(): full_hidden = lax.all_gather(decode_hidden, 'rep', axis=1, tiled=True)  29 us
    convert_element_type x1, other arithmetic, local(): weights.astype(BF16)  9.66 us
    convert_element_type x1, local copies, waits for them, and re-layouts, local(): weights.astype(BF16)  9.03 us
    dot_general x2, matrix products, own_columns(): jnp.dot(normed.reshape(-1, model_width), key_value_weight, preferred_elem...  6.1 us
    dot_general x1, matrix products, local(): jnp.einsum('sthd,pnhd->sthpn', query_matrix, piece_keys, preferred_elemen...  5.74 us
  transfers between devices with their start and end apart: 4, of which 3 were waited for; matrix products, arithmetic and copies ran while one was open for 6% of the time, Pallas kernels for 0%

profile of v1, /device:TPU:513, one launch (start us, length us, event | category | flops | bytes accessed | tf_op | source)
XLA Modules:
  0.0 271.2 jit_solution(7038429710667568036)
XLA Ops:
  6.5 0.0 copy-start
  6.6 0.0 all-gather.2.cloned.1.call-start
  6.6 0.7 all-gather.2.cloned.1.call-update
  7.3 0.1 reduce-scatter.2.cloned.1.call-start
  7.4 1.1 fusion.19
  8.6 1.2 fusion.21
  9.8 1.3 fusion.79
  11.1 0.1 fusion.65
  11.2 0.1 fusion.68
  11.3 2.3 collective-permute-start.1
  13.6 1.5 fusion.78
  15.1 2.7 select_reduce_fusion
  17.8 0.7 iota_compare_fusion
  18.5 0.1 iota_add_fusion
  18.6 0.3 broadcast_and_fusion
  18.9 0.0 collective-permute-done.1
  18.9 0.1 fusion.77
  19.1 35.0 %all_gather.7 = bf16[8,384,1,128]{3,0,2,1:T(8,128)(2,1)S(1)} all-gather(bf16[8,24,1,128]{3,0,2,1:T(8,128)(2,1)S(1)} %copy.186), channel_id=1, replica_groups=mesh['groups'=2,'ep'=16,'rep'=8] {'ep'}, dimensions={1}, use_global_device_ids=true | all-gather | bytes 835584 | tf_op jit(solution)/shard_map/all_gather | solution.py:26
  54.1 0.3 slice_bitcast_fusion
  54.3 0.1 copy.187
  54.4 29.0 %all-gather.2.cloned.1.call-done = bf16[128,8,2048]{2,0,1:T(8,128)(2,1)} async-done(((bf16[128,1,2048]{2,0,1:T(8,128)(2,1)}), bf16[128,8,2048]{2,0,1:T(8,128)(2,1)}) %all-gather.2.cloned.1.call-update) | async-done | bytes 4194320 | tf_op jit(solution)/shard_map/all_gather | solution.py:271
  83.4 4.5 %fusion.3 = f32[128,8]{1,0:T(8,128)S(1)} fusion(bf16[128,8,2048]{2,0,1:T(8,128)(2,1)} %all-gather.2.cloned.1.call-done), kind=kLoop, calls=%fused_computation.8 | loop fusion | flops 6290432 | bytes 4198400 | tf_op jit(solution)/shard_map/reduce_sum | solution.py:45
  88.0 0.1 copy.179
  88.1 0.0 copy-done.7
  88.1 0.0 copy-start.5
  88.1 4.8 %fusion.7 = f32[1024,128]{1,0:T(8,128)S(1)} fusion(bf16[2048,128]{1,0:T(8,128)(2,1)S(1)} %copy-done.4, f32[2048]{0:T(1024)S(1)} %copy-done.7, f32[128,8]{1,0:T(8,128)S(1)} %copy.179, bf16[128,8,2048]{2,0,1:T(8,128)(2,1)} %all-gather.2.cloned.1.call-done), kind=kOutput, calls=%fused_computation.12 | convolution fusion | flops 545259520 | bytes 5255168 | tf_op jit(solution)/shard_map/dot_general | solution.py:289
  92.9 2.4 fusion.34
  95.3 0.2 fusion.38
  95.5 0.3 collective-permute-start
  95.8 5.7 %fusion = (f32[128,8,2]{0,1,2:T(8,128)S(1)}, f32[2,4,384,128,8]{3,2,4,1,0:T(8,128)}) fusion(pred[128,4,384]{0,2,1:T(8,128)(4,1)S(1)} %broadcast_and_fusion, bf16[128,8,2,128,1]{3,1,2,0,4:T(8,128)(2,1)S(1)} %bitcast.133, pred[2]{0:T(512)(128)(4,1)S(1)} %compare_and_fusion.1, bf16[4,384,128]{2,1,0:T(8,128)(2,1)S(1)} %copy.187), kind=kOutput, calls=%fused_computation.3 | convolution fusion | flops 815134720 | bytes 13705218 | tf_op jit(solution)/shard_map/sthd,pnhd->sthpn/dot_general | solution.py:370
  101.6 0.1 copy.192
  101.6 1.2 collective-permute-done
  102.8 0.2 fusion.39
  103.0 0.5 fusion.41
  103.5 0.4 copy.182
  104.0 0.1 fusion.63
  104.1 0.1 fusion.69
  104.2 9.7 %fusion.2 = (bf16[128,8,2,4,384]{0,4,1,3,2:T(8,128)(2,1)}, f32[128,8,2]{0,1,2:T(8,128)S(1)}) fusion(f32[2,4,384,128,8]{3,2,4,1,0:T(8,128)} %get-tuple-element.30, f32[128,8,2]{0,1,2:T(8,128)S(1)} %copy_maximum_fusion, pred[128,4,384]{0,2,1:T(8,128)(4,1)S(1)} %broadcast_and_fusion), kind=kLoop, calls=%fused_computation.7 | loop fusion | flops 18872320 | bytes 19087360 | tf_op jit(solution)/shard_map/convert_element_type | solution.py:379
  113.9 9.0 %copy.193 = bf16[128,8,2,4,384]{4,1,3,2,0:T(8,128)(2,1)} copy(bf16[128,8,2,4,384]{0,4,1,3,2:T(8,128)(2,1)} %get-tuple-element.11) | data formatting | bytes 12582912 | tf_op jit(solution)/shard_map/convert_element_type | solution.py:379
  122.9 0.1 copy.191
  123.1 0.4 copy.185
  123.5 0.1 copy.196
  123.6 0.5 fusion.14
  124.2 4.7 %fusion.16 = bf16[8,128,256]{2,0,1:T(8,128)(2,1)S(1)} fusion(f32[128,8,2,128]{3,1,2,0:T(8,128)S(1)} %fusion.14, bf16[128,8,2,4,384]{4,1,3,2,0:T(8,128)(2,1)} %copy.193, pred[2]{0:T(512)(128)(4,1)S(1)} %compare_and_fusion.1, f32[128,8,2]{1,2,0:T(2,128)S(1)} %copy.196, bf16[4,384,128]{2,1,0:T(8,128)(2,1)S(1)} %copy.192), kind=kOutput, calls=%fused_computation.23 | convolution fusion | flops 806486016 | bytes 8265730 | tf_op jit(solution)/shard_map/sthpn,pnhd->sthd/dot_general | solution.py:377
  128.9 0.0 copy-done
  128.9 0.0 copy-start.8
  128.9 0.0 copy-start.6
  128.9 0.0 copy-start.3
  128.9 0.0 copy-start.2
  128.9 3.2 %convolution_convert_fusion = bf16[8,128,2048]{2,1,0:T(8,128)(2,1)} fusion(bf16[256,2048]{1,0:T(8,128)(2,1)S(1)} %copy-done, bf16[8,128,256]{2,0,1:T(8,128)(2,1)S(1)} %fusion.16), kind=kOutput, calls=%fused_computation.15 | convolution fusion | flops 1075838976 | bytes 5767168 | tf_op jit(solution)/shard_map/dot_general | solution.py:395
  132.1 0.1 reduce-scatter.2.cloned.1.call-update
  132.2 0.1 copy.201
  132.3 0.1 copy.200
  132.4 0.1 copy.199
  132.6 0.1 select_reduce_fusion.1
  132.7 1.1 gather_fusion
  133.9 0.1 copy.202
  134.0 0.1 reduce.1
  134.1 54.6 %reduce-scatter.2.cloned.1.call-done = bf16[1,128,2048]{2,1,0:T(8,128)(2,1)} async-done(((bf16[8,128,2048]{2,1,0:T(8,128)(2,1)}), bf16[1,128,2048]{2,1,0:T(8,128)(2,1)}) %reduce-scatter.2.cloned.1.call-update) | async-done | bytes 524304 | tf_op jit(solution)/shard_map/reduce_scatter | solution.py:394
  188.7 1.2 fusion.37.mixed_ref
  189.9 0.0 copy-start.1
  189.9 1.9 copy-done.1
  191.8 71.7 %moe.1 = bf16[128,2048]{1,0:T(8,128)(2,1)S(1)} custom-call(bf16[128,2048]{1,0:T(8,128)(2,1)S(1)} %fusion.37.mixed_ref, f32[1,2048]{1,0:T(1,128)S(1)} %bitcast.126, s32[1,128]{1,0:T(1,128)S(1)} %bitcast_select_fusion.2.row_ref, s32[128,1]{1,0:T(8,128)S(1)} %get-tuple-element.6.col_ref, bf16[2048,768]{1,0:T(8,128)(2,1)S(1)} %bitcast.124, ...), custom_call_target="tpu_custom_call" | custom-call | tf_op jit(solution)/shard_map/moe/pallas_call | solution.py:235
  263.5 0.8 copy.242
  (31 shorter events, 0.3 us)
Async XLA Ops:
  6.5 122.3 %copy-start = (bf16[256,2048]{1,0:T(8,128)(2,1)S(1)}, bf16[256,2048]{1,0:T(8,128)(2,1)}, u32[]{:S(2)}) copy-start(bf16[256,2048]{1,0:T(8,128)(2,1)} %param.22) | copy-start | bytes 3145732
  6.6 81.6 %copy-start.7 = (f32[2048]{0:T(1024)S(1)}, f32[2048]{0:T(1024)}, u32[]{:S(2)}) copy-start(f32[2048]{0:T(1024)} %param.20) | copy-start | bytes 24580
  6.6 81.6 %copy-start.4 = (bf16[2048,128]{1,0:T(8,128)(2,1)S(1)}, bf16[2048,128]{1,0:T(8,128)(2,1)}, u32[]{:S(2)}) copy-start(bf16[2048,128]{1,0:T(8,128)(2,1)} %param.21) | copy-start | bytes 1572868
  6.6 76.8 %all-gather.2.cloned.1.call-start = ((), (), s32[]{:S(2)}) async-start(), calls=%async_computation.1 | async-start | bytes 4718592 | tf_op jit(solution)/shard_map/all_gather | solution.py:271
  7.3 181.4 %reduce-scatter.2.cloned.1.call-start = ((), (), s32[]{:S(2)}) async-start(), calls=%async_computation.2 | async-start | bytes 4718592 | tf_op jit(solution)/shard_map/reduce_scatter | solution.py:394
  11.3 7.6 %collective-permute-start.1 = (bf16[4,24,128]{2,1,0:T(8,128)(2,1)S(1)}, bf16[4,24,128]{2,1,0:T(8,128)(2,1)S(1)}, u32[]{:S(2)}, u32[]{:S(2)}) collective-permute-start(bf16[4,24,128]{2,1,0:T(8,128)(2,1)S(1)} %fusion.68), channel_id=1, source_target_pairs={{0,1},{1,0},{2,3},{3,2},{4,5},{5,4},{6,7},{7,6},{8,9},{9,8},{10,11... | collective-permute-start | bytes 73736 | tf_op jit(solution)/shard_map/ppermute | solution.py:40
  88.1 7.7 %copy-start.5 = (bf16[128,8,256]{2,1,0:T(8,128)(2,1)S(1)}, bf16[128,8,256]{2,1,0:T(8,128)(2,1)}, u32[]{:S(2)}) copy-start(bf16[128,8,256]{2,1,0:T(8,128)(2,1)} %param.19) | copy-start | bytes 1572868
  95.5 7.3 %collective-permute-start = (bf16[128,8,128]{2,1,0:T(8,128)(2,1)S(1)}, bf16[128,8,128]{2,1,0:T(8,128)(2,1)S(1)}, u32[]{:S(2)}, u32[]{:S(2)}) collective-permute-start(bf16[128,8,128]{2,1,0:T(8,128)(2,1)S(1)} %fusion.38), channel_id=1, source_target_pairs={{0,1},{1,0},{2,3},{3,2},{4,5},{5,4},{6,7},{7,6},{8,9},{9,8},{10,11... | collective-permute-start | bytes 786440 | tf_op jit(solution)/shard_map/ppermute | solution.py:40
  128.9 3.3 %copy-start.8 = (s32[128,1]{0,1:T(1,128)S(1)}, s32[128,1]{0,1:T(1,128)}, u32[]{:S(2)}) copy-start(s32[128,1]{0,1:T(1,128)} %param.28) | copy-start | bytes 1540
  128.9 3.8 %copy-start.6 = (s32[151936]{0:T(1024)S(1)}, s32[151936]{0:T(1024)}, u32[]{:S(2)}) copy-start(s32[151936]{0:T(1024)} %param.27) | copy-start | bytes 1823236
  128.9 59.8 %copy-start.3 = (bf16[128,1,2048]{2,0,1:T(8,128)(2,1)S(1)}, bf16[128,1,2048]{2,0,1:T(8,128)(2,1)}, u32[]{:S(2)}) copy-start(bf16[128,1,2048]{2,0,1:T(8,128)(2,1)} %param.18) | copy-start | bytes 1572868
  128.9 61.0 %copy-start.2 = (f32[2048]{0:T(1024)S(1)}, f32[2048]{0:T(1024)}, u32[]{:S(2)}) copy-start(f32[2048]{0:T(1024)} %param.23) | copy-start | bytes 24580
  189.9 1.9 copy-start.1
Sparse Core Ops, SparseCore 0:
  9.2 74.2 all-gather.1
  132.3 56.3 reduce-scatter.1

commit v2 on v1

v2 whole, which is shorter than its diff:
```python
import functools
import math

import jax
import jax.numpy as jnp
from jax import lax
from jax.experimental import pallas as pl
from jax.experimental.pallas import tpu as pltpu
from jax.sharding import PartitionSpec as P

HEAD_DIM = 128
QUERY_HEADS = 16
KEY_VALUE_HEADS = 4
GROUP_PROMPTS = 4
CAP = 2

EPS = 1e-06
THETA = 1000000.0
MESH = pl.DeviceIdType.MESH
F32 = jnp.float32
BF16 = jnp.bfloat16


def dot(a, b):
    return jnp.dot(a, b, preferred_element_type=F32)


def dot_t(a, b):
    return lax.dot_general(a, b, (((0,), (0,)), ((), ())), preferred_element_type=F32)


def one_hot(hit):
    return jnp.where(hit, 1.0, 0.0).astype(BF16)


def moe_kernel(
    nx, ne, mixed_ref, gain_ref, row_ref, col_ref, gate_hbm, up_hbm, down_hbm, out_ref,
    gate, up, down, normed, xin, hid,
    s0, s1, r0, r1, t0, t1, q0, q1, o0, o1, b0, b1, c0, c1, f0, f1,
    wsem, ssem, rsem,
):
    e, x, g = lax.axis_index("ep"), lax.axis_index("rep"), lax.axis_index("groups")
    rows, width = mixed_ref.shape
    ff = gate.shape[1]
    half = nx * ne
    loads = [
        pltpu.make_async_copy(gate_hbm, gate, wsem.at[0]),
        pltpu.make_async_copy(up_hbm, up, wsem.at[1]),
        pltpu.make_async_copy(down_hbm, down, wsem.at[2]),
    ]
    for load in loads:
        load.start()
    barrier = pltpu.get_barrier_semaphore()
    for i in range(1, nx):
        peer = (g, e, lax.rem(x + i, nx))
        pl.semaphore_signal(barrier, inc=1, device_id=peer, device_id_type=MESH)
    for i in range(1, ne):
        peer = (g, lax.rem(e + i, ne), x)
        pl.semaphore_signal(barrier, inc=1, device_id=peer, device_id_type=MESH)

    widened = mixed_ref[...].astype(F32)
    scale = lax.rsqrt(jnp.mean(widened * widened, axis=-1, keepdims=True) + EPS)
    normed[...] = (widened * scale * gain_ref[...]).astype(BF16)

    row, col = row_ref[...], col_ref[...]
    first = lax.broadcasted_iota(jnp.int32, (rows, rows), 0)
    second = lax.broadcasted_iota(jnp.int32, (rows, rows), 1)
    earlier = jnp.where((row == col) & (first < second), 1, 0)
    rank = jnp.sum(earlier, axis=0, keepdims=True)
    slot = lax.broadcasted_iota(jnp.int32, (half, rows), 0)
    turned = lax.rem(slot, ne) * nx + slot // ne
    pick0 = one_hot((turned == row) & (rank == 0))
    pick1 = one_hot((slot == row) & (rank == 1))

    here = lax.broadcasted_iota(jnp.int32, (half, half), 0)
    there = lax.broadcasted_iota(jnp.int32, (half, half), 1)
    to_ex = one_hot(there == lax.rem(here, nx) * ne + here // nx)
    to_xe = one_hot(there == lax.rem(here, ne) * nx + here // ne)

    tile = 512

    def over_columns(body):
        def step(i, carry):
            body(pl.ds(pl.multiple_of(i * tile, tile), tile))
            return carry

        lax.fori_loop(0, width // tile, step, 0)

    def put(ref, cols, value):
        ref[:, :, cols] = value.reshape(ref.shape[0], ref.shape[1], tile).astype(BF16)

    def get(ref, cols):
        return ref[:, :, cols].astype(F32).reshape(half, tile).astype(BF16)

    def send_x(src, dst, k):
        for i in range(1, nx):
            to = lax.rem(x + i, nx)
            pltpu.make_async_remote_copy(
                src.at[to], dst.at[x], ssem.at[k], rsem.at[k],
                device_id=(g, e, to), device_id_type=MESH,
            ).start()

    def send_e(src, dst, k):
        for i in range(1, ne):
            to = lax.rem(e + i, ne)
            pltpu.make_async_remote_copy(
                src.at[to], dst.at[e], ssem.at[k], rsem.at[k],
                device_id=(g, to, x), device_id_type=MESH,
            ).start()

    def arrive(src, dst, k):
        n = dst.shape[0] - 1
        pltpu.make_async_copy(src.at[pl.ds(0, n)], dst.at[pl.ds(0, n)], ssem.at[k]).wait()
        pltpu.make_async_copy(src.at[pl.ds(0, n)], dst.at[pl.ds(0, n)], rsem.at[k]).wait()

    def scatter(cols):
        put(s0, cols, dot(pick0, normed[:, cols]))
        put(s1, cols, dot(pick1, normed[:, cols]))

    over_columns(scatter)
    pl.semaphore_wait(barrier, nx + ne - 2)
    send_x(s0, r0, 0)
    send_e(s1, r1, 1)
    r0[x] = s0[x]
    r1[e] = s1[e]
    arrive(s0, r0, 0)
    over_columns(lambda cols: put(t0, cols, dot(to_ex, get(r0, cols))))
    send_e(t0, q0, 2)
    q0[e] = t0[e]
    arrive(s1, r1, 1)
    over_columns(lambda cols: put(t1, cols, dot(to_xe, get(r1, cols))))
    send_x(t1, q1, 3)
    q1[x] = t1[x]

    for load in loads:
        load.wait()
    arrive(t0, q0, 2)
    arrive(t1, q1, 3)

    def collect(cols):
        xin[pl.ds(0, half), cols] = get(q0, cols)
        xin[pl.ds(half, half), cols] = get(q1, cols)

    over_columns(collect)
    ftile = 256

    def inner(i, carry):
        cols = pl.ds(pl.multiple_of(i * ftile, ftile), ftile)
        gate_proj = dot(xin[...], gate[:, cols])
        up_proj = dot(xin[...], up[:, cols])
        hid[:, cols] = (jax.nn.silu(gate_proj) * up_proj).astype(BF16)
        return carry

    lax.fori_loop(0, ff // ftile, inner, 0)

    def outer(cols):
        put(o0, cols, dot(hid[pl.ds(0, half), :], down[:, cols]))
        put(o1, cols, dot(hid[pl.ds(half, half), :], down[:, cols]))

    over_columns(outer)
    send_e(o0, b0, 4)
    send_x(o1, b1, 5)
    b0[e] = o0[e]
    b1[x] = o1[x]
    arrive(o0, b0, 4)
    over_columns(lambda cols: put(c0, cols, dot(to_xe, get(b0, cols))))
    send_x(c0, f0, 6)
    f0[x] = c0[x]
    arrive(o1, b1, 5)
    over_columns(lambda cols: put(c1, cols, dot(to_ex, get(b1, cols))))
    send_e(c1, f1, 7)
    f1[e] = c1[e]
    arrive(c0, f0, 6)
    arrive(c1, f1, 7)

    def combine(cols):
        moe = dot_t(pick0, get(f0, cols)) + dot_t(pick1, get(f1, cols))
        out_ref[:, cols] = (mixed_ref[:, cols].astype(F32) + moe).astype(BF16)

    over_columns(combine)


def moe(mixed, gain, row, col, gate_weight, up_weight, down_weight):
    nx, ne = lax.axis_size("rep"), lax.axis_size("ep")
    rows, width = mixed.shape
    ff = gate_weight.shape[2]
    half = nx * ne
    xe = pltpu.VMEM((nx, ne, width), BF16)
    ex = pltpu.VMEM((ne, nx, width), BF16)
    vmem, any_ = pl.BlockSpec(memory_space=pltpu.VMEM), pl.BlockSpec(memory_space=pl.ANY)
    return pl.pallas_call(
        functools.partial(moe_kernel, nx, ne),
        out_shape=jax.ShapeDtypeStruct((rows, width), BF16),
        in_specs=[vmem] * 4 + [any_] * 3,
        out_specs=vmem,
        scratch_shapes=[
            pltpu.VMEM((width, ff), BF16), pltpu.VMEM((width, ff), BF16), pltpu.VMEM((ff, width), BF16),
            pltpu.VMEM((rows, width), BF16), pltpu.VMEM((2 * half, width), BF16), pltpu.VMEM((2 * half, ff), BF16),
            xe, ex, xe, ex, ex, xe, ex, xe, ex, xe, ex, xe, xe, ex, xe, ex,
            pltpu.SemaphoreType.DMA((3,)), pltpu.SemaphoreType.DMA((8,)), pltpu.SemaphoreType.DMA((8,)),
        ],
        compiler_params=pltpu.CompilerParams(
            collective_id=1, has_side_effects=True, vmem_limit_bytes=48 << 20
        ),
        name="moe",
    )(
        mixed, gain.reshape(1, width), row, col,
        gate_weight[0], up_weight[0], down_weight[0],
    )


SHARED_ROWS = 1280


def front_kernel(
    nx, ne, prompt_ref, hidden_ref, query_ref, gain_ref, lengths_ref, ids_ref, idcol_ref,
    kvw_hbm, ow_hbm, table_hbm, mixed_ref, col_ref, row_ref,
    kvw, ow, table, picked, hn, pn, qf, qt, skv, dkv, spk, pkv, pf, kp, vp, att, full,
    lsem, ring_send, ring_recv, dd_send, dd_recv, xs, xr,
):
    e, x, g = lax.axis_index("ep"), lax.axis_index("rep"), lax.axis_index("groups")
    ny = ne // 2
    y, c = e // 2, lax.rem(e, 2)
    rows, width = hidden_ref.shape
    shared = SHARED_ROWS
    piece = shared // ne
    sub = (width - shared) // 4
    orow = ow.shape[1] // ne
    half = ow.shape[2] // 2
    plen = prompt_ref.shape[0] // GROUP_PROMPTS
    own_prompt = e // (ne // GROUP_PROMPTS)
    seqs = 16

    def sub_rows(core, s):
        start = pl.multiple_of(shared + core * (2 * sub) + s * sub, 16)
        return pl.ds(start, sub)

    def piece_rows(k, size, unit):
        return pl.ds(pl.multiple_of(k * unit, 16), size)

    loads = [
        pltpu.make_async_copy(
            kvw_hbm.at[pl.ds(shared, width - shared)], kvw.at[x, pl.ds(shared, width - shared)], lsem.at[0]
        ),
        pltpu.make_async_copy(
            kvw_hbm.at[piece_rows(e, piece, piece)], kvw.at[x, piece_rows(e, piece, piece)], lsem.at[1]
        ),
        pltpu.make_async_copy(
            ow_hbm.at[piece_rows(e, orow, orow)], ow.at[x, piece_rows(e, orow, orow)], lsem.at[2]
        ),
        pltpu.make_async_copy(table_hbm, table, lsem.at[3]),
    ]
    for load in loads:
        load.start()

    sibling = (g, 2 * y + 1 - c, x)

    def at_x(k):
        return (g, e, lax.rem(x + k + nx, nx))

    def at_y(k):
        return (g, 2 * lax.rem(y + k + ny, ny) + c, x)

    barrier = pltpu.get_barrier_semaphore()
    for i in range(1, nx):
        pl.semaphore_signal(barrier, inc=1, device_id=at_x(i), device_id_type=MESH)
    for i in range(1, ny):
        pl.semaphore_signal(barrier, inc=1, device_id=at_y(i), device_id_type=MESH)
    pl.semaphore_signal(barrier, inc=1, device_id=sibling, device_id_type=MESH)

    class Ring:
        def __init__(self, number, along, sign, hops, chunk, total, mate):
            self.along, self.sign, self.hops, self.chunk = along, sign, hops, chunk
            self.number, self.total, self.mate = number, total, mate

        def origin(self, h):
            me, n = (x, nx) if self.along == "x" else (y, ny)
            return lax.rem(me - self.sign * h + n, n)

        def go(self, h):
            ref = self.chunk(self.origin(h))
            to = at_x(self.sign) if self.along == "x" else at_y(self.sign)
            pltpu.make_async_remote_copy(
                ref, ref, ring_send.at[self.number], ring_recv.at[self.number, h],
                device_id=to, device_id_type=MESH,
            ).start()

        def event(self, h):
            if h > self.hops:
                return
            ref = self.chunk(self.origin(h))
            pltpu.make_async_copy(ref, ref, ring_recv.at[self.number, h - 1]).wait()
            if h < self.hops:
                self.go(h)
            if self.mate is not None:
                to_mate(ref, self.mate)

        def finish(self):
            ref = self.total(self.hops)
            pltpu.make_async_copy(ref, ref, ring_send.at[self.number]).wait()

    def to_mate(ref, k):
        pltpu.make_async_remote_copy(
            ref, ref, dd_send.at[k], dd_recv.at[k], device_id=sibling, device_id_type=MESH
        ).start()

    def mate_done(ref, k):
        pltpu.make_async_copy(ref, ref, dd_send.at[k]).wait()
        pltpu.make_async_copy(ref, ref, dd_recv.at[k]).wait()

    def rings(base, along, chunk, total, mate):
        made = []
        for s in range(2):
            for sign in (1, -1):
                hops = 4 if (s == 0) == (sign == 1) else 3
                made.append(
                    Ring(
                        base + len(made), along, sign, hops,
                        functools.partial(chunk, s), functools.partial(total, s), mate,
                    )
                )
        return made

    kv_x = rings(
        0, "x",
        lambda s, k: kvw.at[k, sub_rows(c, s)],
        lambda s, n: kvw.at[pl.ds(0, n), sub_rows(0, s)],
        0,
    )
    kv_y = rings(
        4, "y",
        lambda s, k: kvw.at[pl.ds(4 * s, 4), piece_rows(2 * k + c, piece, piece)],
        lambda s, n: kvw.at[pl.ds(4 * s, 4), pl.ds(0, n * piece)],
        1,
    )
    ow_x = rings(
        8, "x",
        lambda s, k: ow.at[k, piece_rows(e, orow, orow), pl.ds(s * half, half)],
        lambda s, n: ow.at[pl.ds(0, n), pl.ds(0, orow), pl.ds(s * half, half)],
        None,
    )
    ow_y = rings(
        12, "y",
        lambda s, k: ow.at[pl.ds(4 * s, 4), piece_rows(2 * k + c, orow, orow)],
        lambda s, n: ow.at[pl.ds(4 * s, 4), pl.ds(0, n * orow)],
        2,
    )

    def normalised(ref, out):
        widened = ref[...].astype(F32)
        scale = lax.rsqrt(jnp.mean(widened * widened, axis=-1, keepdims=True) + EPS)
        out[...] = (widened * scale * gain_ref[...]).astype(BF16)

    for load in loads:
        load.wait()
    pl.semaphore_wait(barrier, nx + ny - 1)

    own_piece = piece_rows(e, piece, piece)
    for i in range(1, nx):
        ref = kvw.at[x, own_piece]
        pltpu.make_async_remote_copy(
            ref, ref, xs.at[0], xr.at[0], device_id=at_x(i), device_id_type=MESH
        ).start()
    for ring in kv_x:
        ring.go(0)
    for ring in ow_x:
        ring.go(0)
    normalised(hidden_ref, hn)
    ref = kvw.at[pl.ds(0, nx - 1), pl.ds(0, piece)]
    pltpu.make_async_copy(ref, ref, xs.at[0]).wait()
    pltpu.make_async_copy(ref, ref, xr.at[0]).wait()
    for ring in kv_y:
        ring.go(0)
    for s in range(2):
        to_mate(kvw.at[pl.ds(4 * s, 4), own_piece], 1)

    for h in range(1, 5):
        for ring in kv_x:
            ring.event(h)
        for ring in kv_y:
            ring.event(h)
        for ring in ow_x:
            ring.event(h)
        if h == 1:
            normalised(prompt_ref, pn)
            for k in range(2):
                qf[k] = query_ref[:, pl.ds(k * HEAD_DIM, HEAD_DIM)].astype(F32)
        if h == 2:
            for t in range(nx):
                for k in range(2):
                    cols = pl.ds(k * HEAD_DIM, HEAD_DIM)
                    qt[t, :, cols] = qf[k, pl.ds(t, rows, stride=nx), :].astype(BF16)
        if h == 3:
            def look(i, carry):
                at = lax.div(ids_ref[i], 128)
                picked[pl.ds(i, 1), :] = table[pl.ds(at, 1), :]
                return carry

            lax.fori_loop(0, rows, look, 0)
            lane = lax.broadcasted_iota(jnp.int32, (rows, 128), 1)
            line = lax.broadcasted_iota(jnp.int32, (rows, 128), 0)
            chosen = jnp.sum(
                jnp.where(lane == lax.rem(idcol_ref[...], 128), picked[...], 0), axis=1, keepdims=True
            )
            col_ref[...] = chosen
            row_ref[...] = jnp.sum(jnp.where(lane == line, chosen, 0), axis=0, keepdims=True)
    mate_done(kvw.at[pl.ds(0, nx - 1), pl.ds(0, 2 * sub)], 0)
    mate_done(kvw.at[pl.ds(0, nx), pl.ds(0, ny * piece)], 1)

    length = lengths_ref[own_prompt]
    half_dim = HEAD_DIM // 2

    def turns(count, positions):
        lane = lax.broadcasted_iota(jnp.int32, (count, HEAD_DIM), 1)
        freq = jnp.exp(lax.rem(lane, half_dim).astype(F32) * (-2.0 * math.log(THETA) / HEAD_DIM))
        angles = positions.astype(F32) * freq
        sine = jnp.sin(angles)
        return jnp.cos(angles), jnp.where(lane < half_dim, -sine, sine)

    def turned(keys, cosine, sine):
        return keys * cosine + pltpu.roll(keys, half_dim, 1) * sine

    cosine, sine = turns(8, jnp.full((8, HEAD_DIM), length + x, jnp.int32))
    cosine, sine = cosine[0:1], sine[0:1]
    for head in range(KEY_VALUE_HEADS):
        skv[head, 0] = turned(dot(hn[...], kvw[2 * head]), cosine, sine).astype(BF16)
        skv[head, 1] = dot(hn[...], kvw[2 * head + 1]).astype(BF16)
    for i in range(1, nx):
        to = lax.rem(x + i, nx)
        pltpu.make_async_remote_copy(
            skv.at[to // 2], dkv.at[x], xs.at[1], xr.at[1], device_id=(g, e, to), device_id_type=MESH
        ).start()
    dkv[x] = skv[x // 2]

    count = GROUP_PROMPTS * plen
    line = lax.broadcasted_iota(jnp.int32, (count, HEAD_DIM), 0)
    pcos, psin = turns(count, e * plen + lax.rem(line, plen))
    head = x // 2
    pkey = turned(dot(pn[...], kvw[2 * head]), pcos, psin)
    pval = dot(pn[...], kvw[2 * head + 1])
    spk[:, 0] = pkey.reshape(GROUP_PROMPTS, plen, HEAD_DIM).astype(BF16)
    spk[:, 1] = pval.reshape(GROUP_PROMPTS, plen, HEAD_DIM).astype(BF16)
    per = ny // GROUP_PROMPTS
    for i in range(1, ny):
        to = lax.rem(y + i, ny)
        pltpu.make_async_remote_copy(
            spk.at[to // per], pkv.at[c, y], xs.at[2], xr.at[2],
            device_id=(g, 2 * to + c, x), device_id_type=MESH,
        ).start()
    pkv[c, y] = spk[y // per]
    for ring in ow_y:
        ring.go(0)
    for s in range(2):
        to_mate(ow.at[pl.ds(4 * s, 4), piece_rows(e, orow, orow)], 2)

    ref = pkv.at[0, pl.ds(0, ny - 1)]
    pltpu.make_async_copy(ref, ref, xs.at[2]).wait()
    pltpu.make_async_copy(ref, ref, xr.at[2]).wait()
    to_mate(pkv.at[c], 3)
    mate_done(pkv.at[0], 3)
    for k in range(2):
        for core in range(2):
            for row in range(ny):
                start = (2 * row + core) * plen
                pf[pl.ds(start, plen), :] = pkv[core, row, k].astype(F32)
        (kp if k == 0 else vp)[...] = pf[...].astype(BF16)

    for ring in ow_y:
        ring.event(1)

    ref = dkv.at[pl.ds(0, nx - 1)]
    pltpu.make_async_copy(ref, ref, xs.at[1]).wait()
    pltpu.make_async_copy(ref, ref, xr.at[1]).wait()

    keys = kp.shape[0]
    block = 2 * nx * seqs
    scale = HEAD_DIM ** (-0.5)
    valid = lax.broadcasted_iota(jnp.int32, (block, keys), 1) < length
    r = lax.rem(lax.broadcasted_iota(jnp.int32, (block, nx * seqs), 0), nx * seqs)
    k = lax.broadcasted_iota(jnp.int32, (block, nx * seqs), 1)
    own = (lax.rem(r, seqs) == lax.rem(k, seqs)) & (k // seqs <= r // seqs)

    def nt(a, b):
        return lax.dot_general(a, b, (((1,), (1,)), ((), ())), preferred_element_type=F32)

    def attend(j, carry):
        pick = pl.ds(pl.multiple_of(j * seqs, seqs), seqs)
        q2 = jnp.concatenate(
            [qt[:, pick, pl.ds(h * HEAD_DIM, HEAD_DIM)].reshape(nx * seqs, HEAD_DIM) for h in range(2)], axis=0
        )
        sp = jnp.where(valid, nt(q2, kp[...]) * scale, -1e30)
        sd = jnp.where(own, nt(q2, dkv[:, 0, pick].reshape(nx * seqs, HEAD_DIM)) * scale, -1e30)
        top = jnp.maximum(jnp.max(sp, axis=1, keepdims=True), jnp.max(sd, axis=1, keepdims=True))
        wp = jnp.where(valid, jnp.exp(sp - top), 0.0)
        wd = jnp.where(own, jnp.exp(sd - top), 0.0)
        total = jnp.sum(wp, axis=1, keepdims=True) + jnp.sum(wd, axis=1, keepdims=True)
        summed = dot(wp.astype(BF16), vp[...])
        summed = summed + dot(wd.astype(BF16), dkv[:, 1, pick].reshape(nx * seqs, HEAD_DIM))
        result = (summed / total).astype(BF16)
        for h in range(2):
            att[:, pick, pl.ds(h * HEAD_DIM, HEAD_DIM)] = result[h * nx * seqs:(h + 1) * nx * seqs].reshape(
                nx, seqs, HEAD_DIM
            )
        return carry

    lax.fori_loop(0, rows // seqs, attend, 0)
    for i in range(1, nx):
        to = lax.rem(x + i, nx)
        pltpu.make_async_remote_copy(
            att.at[to], full.at[x], xs.at[3], xr.at[3], device_id=(g, e, to), device_id_type=MESH
        ).start()
    full[x] = att[x]
    for h in range(2, 5):
        for ring in ow_y:
            ring.event(h)
    ref = full.at[pl.ds(0, nx - 1)]
    pltpu.make_async_copy(ref, ref, xs.at[3]).wait()
    pltpu.make_async_copy(ref, ref, xr.at[3]).wait()
    mate_done(ow.at[pl.ds(0, nx), pl.ds(0, ny * orow)], 2)

    tile = 512

    def project(i, carry):
        cols = pl.ds(pl.multiple_of(i * tile, tile), tile)
        total = dot(full[0], ow[0, :, cols])
        for k in range(1, nx):
            total = total + dot(full[k], ow[k, :, cols])
        mixed_ref[:, cols] = (hidden_ref[:, cols].astype(F32) + total).astype(BF16)
        return carry

    lax.fori_loop(0, width // tile, project, 0)
    for ring in kv_x + kv_y + ow_x + ow_y:
        ring.finish()


def front(prompt, hidden, queries, gain, lengths, ids, kvw, ow, expert_table):
    nx, ne = lax.axis_size("rep"), lax.axis_size("ep")
    rows, width = hidden.shape
    count = prompt.shape[0]
    plen = count // GROUP_PROMPTS
    keys = plen * ne
    vmem, any_ = pl.BlockSpec(memory_space=pltpu.VMEM), pl.BlockSpec(memory_space=pl.ANY)
    smem = pl.BlockSpec(memory_space=pltpu.SMEM)
    cols = queries.shape[1]
    table = expert_table.reshape(-1, 128)
    sem = pltpu.SemaphoreType.DMA
    return pl.pallas_call(
        functools.partial(front_kernel, nx, ne),
        out_shape=(
            jax.ShapeDtypeStruct((rows, width), BF16),
            jax.ShapeDtypeStruct((rows, 1), jnp.int32),
            jax.ShapeDtypeStruct((1, rows), jnp.int32),
        ),
        in_specs=[vmem] * 4 + [smem] * 2 + [vmem] + [any_] * 3,
        out_specs=(vmem, vmem, vmem),
        scratch_shapes=[
            pltpu.VMEM((nx,) + kvw.shape, BF16),
            pltpu.VMEM((nx,) + ow.shape, BF16),
            pltpu.VMEM(table.shape, jnp.int32),
            pltpu.VMEM((rows, 128), jnp.int32),
            pltpu.VMEM((rows, width), BF16),
            pltpu.VMEM((count, width), BF16),
            pltpu.VMEM((2, queries.shape[0], HEAD_DIM), F32),
            pltpu.VMEM((nx, rows, cols), BF16),
            pltpu.VMEM((KEY_VALUE_HEADS, 2, rows, HEAD_DIM), BF16),
            pltpu.VMEM((nx, 2, rows, HEAD_DIM), BF16),
            pltpu.VMEM((GROUP_PROMPTS, 2, plen, HEAD_DIM), BF16),
            pltpu.VMEM((2, ne // 2, 2, plen, HEAD_DIM), BF16),
            pltpu.VMEM((keys, HEAD_DIM), F32),
            pltpu.VMEM((keys, HEAD_DIM), BF16),
            pltpu.VMEM((keys, HEAD_DIM), BF16),
            pltpu.VMEM((nx, rows, cols), BF16),
            pltpu.VMEM((nx, rows, cols), BF16),
            sem((4,)), sem((16,)), sem((16, 4)), sem((4,)), sem((4,)), sem((4,)), sem((4,)),
        ],
        compiler_params=pltpu.CompilerParams(
            collective_id=0, has_side_effects=True, vmem_limit_bytes=48 << 20
        ),
        name="front",
    )(
        prompt, hidden, queries, gain.reshape(1, width), lengths, ids.reshape(rows), ids.reshape(rows, 1),
        kvw, ow, table,
    )


def local(
    prompt_hidden,
    decode_hidden,
    queries,
    attn_gain,
    key_value_weight,
    out_weight,
    moe_gain,
    gate_weight,
    up_weight,
    down_weight,
    expert_table,
    token_ids,
    prompt_lengths,
):
    rows = decode_hidden.shape[0] * decode_hidden.shape[1]
    width = decode_hidden.shape[2]
    mixed, col, row = front(
        prompt_hidden.reshape(-1, width),
        decode_hidden.reshape(rows, width),
        queries.reshape(-1, queries.shape[2]),
        attn_gain,
        prompt_lengths,
        token_ids,
        key_value_weight,
        out_weight,
        expert_table,
    )
    out = moe(mixed, moe_gain, row, col, gate_weight, up_weight, down_weight)
    return out.reshape(decode_hidden.shape)


def solution(mesh):
    placed = (
        P("groups", "ep", None),
        P(("groups", "ep"), "rep", None),
        P(("groups", "ep"), None, "rep"),
        P(),
        P(None, "rep"),
        P("rep", None),
        P(),
        P(("ep", "rep"), None, None),
        P(("ep", "rep"), None, None),
        P(("ep", "rep"), None, None),
        P(),
        P("ep", "rep"),
        P("groups"),
    )
    return jax.shard_map(
        local,
        mesh=mesh,
        in_specs=placed,
        out_specs=P(("groups", "ep"), "rep", None),
        check_vma=False,
    )
```

time: 272 us -> 178 us (0.65)
  Pallas kernels: 71.7 us -> 168 us
  waiting for transfers between devices: 85.6 us -> 0 us
  blocking collectives: 35 us -> 0 us
  other arithmetic: 24.9 us -> 0 us
  matrix products: 20.7 us -> 0 us
  between operations: 13.9 us -> 0.05 us
  local copies, waits for them, and re-layouts: 16.7 us -> 10.2 us
    pallas_call x0 -> x1, Pallas kernels: none -> 98.7 us  [front(): pl.pallas_call(functools.partial(front_kernel, nx, ne), out_shape=(jax.Sh...]
    reduce_scatter x1 -> x0, waiting for transfers between devices: 54.6 us -> none  [local(): lax.psum_scatter(jnp.dot(by_step.reshape(-1, by_step.shape[-1]), out_weig...]
    all_gather x1 -> x0, blocking collectives: 35 us -> none  [in_one_piece(): filled, at, outs = (lax.all_gather(both, axis, axis=dim, tiled=True), 0, [])]
    all_gather x1 -> x0, waiting for transfers between devices: 29 us -> none  [local(): full_hidden = lax.all_gather(decode_hidden, 'rep', axis=1, tiled=True)]
    dot_general x7 -> x0, matrix products: 20.7 us -> none  [the longest x2 6.1 us: own_columns(): jnp.dot(normed.reshape(-1, model_width), key_value_weight, preferred_elem...]
    convert_element_type x6 -> x0, other arithmetic: 11.1 us -> none  [the longest x1 9.66 us: local(): weights.astype(BF16)]
    convert_element_type x2 -> x0, local copies, waits for them, and re-layouts: 9.46 us -> none  [the longest x1 9.03 us: local(): weights.astype(BF16)]
    unnamed x21 -> x24, local copies, waits for them, and re-layouts: 2.85 us -> 10.2 us
  transfers between devices with their start and end apart: 4 -> 0, of which waited for: 3 -> 0; matrix products, arithmetic and copies ran while one was open for 6% -> 0% of each run, Pallas kernels for 0% -> 0%
where the time goes in v2:
time: 178 us
  Pallas kernels  168 us (94%)
  local copies, waits for them, and re-layouts  10.2 us (6%)
    pallas_call x1, Pallas kernels, front(): pl.pallas_call(functools.partial(front_kernel, nx, ne), out_shape=(jax.Sh...  98.7 us
    pallas_call x1, Pallas kernels, moe(): pl.pallas_call(functools.partial(moe_kernel, nx, ne), out_shape=jax.Shape...  69.1 us
    unnamed x24, local copies, waits for them, and re-layouts  10.2 us

profile of v2, /device:TPU:513, one launch (start us, length us, event | category | flops | bytes accessed | tf_op | source)
XLA Modules:
  0.0 178.1 jit_solution(10264712646295929200)
XLA Ops:
  0.0 0.0 copy-start
  0.0 0.9 copy.14.idcol_ref
  0.9 0.0 copy-start.1
  0.9 1.3 copy-done.1
  2.2 0.0 copy-start.2
  2.2 1.1 copy-done.2
  3.3 0.0 copy-start.3
  3.3 1.0 copy-done.3
  4.3 0.0 copy-start.4
  4.3 1.0 copy-done.4
  5.3 0.0 copy-start.5
  5.3 1.0 copy-done.5
  6.4 0.0 copy-start.6
  6.4 1.0 copy-done.6
  7.4 0.0 copy-start.7
  7.4 0.7 copy-done.7
  8.1 0.0 copy-start.9
  8.1 0.7 copy-done.9
  8.7 0.0 copy-start.10
  8.7 0.7 copy-done.10
  9.4 0.0 copy-start.8
  9.4 98.7 %front.1 = (bf16[128,2048]{1,0:T(8,128)(2,1)S(1)}, s32[128,1]{1,0:T(8,128)S(1)}, s32[1,128]{1,0:T(1,128)S(1)}) custom-call(bf16[96,2048]{1,0:T(8,128)(2,1)S(1)} %bitcast.16, bf16[128,2048]{1,0:T(8,128)(2,1)S(1)} %bitcast.14, bf16[1024,256]{1,0:T(8,128)(2,1)S(1)} %bitcast.15, f32[1,2048]{1,0:T(1,128)S(1)} %bitcast.17, s32[4]{0:T(128)S(1)} %copy-done.10, ...), custom_call_target="tpu_custom_call" | custom-call | tf_op jit(solution)/shard_map/front/pallas_call | solution.py:547
  108.1 0.0 copy-done
  108.1 0.0 copy-done.8
  108.2 69.1 %moe.1 = bf16[128,2048]{1,0:T(8,128)(2,1)S(1)} custom-call(bf16[128,2048]{1,0:T(8,128)(2,1)S(1)} %get-tuple-element.8.mixed_ref, f32[1,2048]{1,0:T(1,128)S(1)} %bitcast.18, s32[1,128]{1,0:T(1,128)S(1)} %get-tuple-element.9.row_ref, s32[128,1]{1,0:T(8,128)S(1)} %get-tuple-element.10.col_ref, bf16[2048,768]{1,0:T(8,128)(2,1)S(1)} %bitcast.11, ...), custom_call_target="tpu_custom_call" | custom-call | tf_op jit(solution)/shard_map/moe/pallas_call | solution.py:191
  177.3 0.8 copy.16
Async XLA Ops:
  0.0 108.1 %copy-start = (bf16[1,2048,768]{2,1,0:T(8,128)(2,1)S(1)}, bf16[1,2048,768]{2,1,0:T(8,128)(2,1)}, u32[]{:S(2)}) copy-start(bf16[1,2048,768]{2,1,0:T(8,128)(2,1)} %param.20) | copy-start | bytes 9437188
  0.9 1.3 copy-start.1
  2.2 1.1 copy-start.2
  3.3 1.0 copy-start.3
  4.3 1.0 copy-start.4
  5.3 1.0 copy-start.5
  6.4 1.0 copy-start.6
  7.4 0.7 copy-start.7
  8.1 0.7 copy-start.9
  8.7 0.7 copy-start.10
  9.4 98.8 %copy-start.8 = (f32[2048]{0:T(1024)S(1)}, f32[2048]{0:T(1024)}, u32[]{:S(2)}) copy-start(f32[2048]{0:T(1024)} %param.19) | copy-start | bytes 24580

commit v3 on v2

--- a/solution.py
+++ b/solution.py
@@ -33,201 +33,29 @@
     return jnp.where(hit, 1.0, 0.0).astype(BF16)
 
 
-def moe_kernel(
-    nx, ne, mixed_ref, gain_ref, row_ref, col_ref, gate_hbm, up_hbm, down_hbm, out_ref,
-    gate, up, down, normed, xin, hid,
+SHARED_ROWS = 1280
+CHUNKS = 2
+
+
+def layer_kernel(
+    nx, ne, prompt_hbm, hidden_hbm, query_hbm, gain_ref, moe_gain_ref, lengths_ref, ids_ref, idrow_ref,
+    kvw_hbm, ow_hbm, table_hbm, gate_hbm, up_hbm, down_hbm, out_ref,
+    prompt_ref, hidden_ref, query_ref,
+    kvw, ow, table, picked, hn, pn, qf, qt, skv, dkv, spk, pkv, pf, kp, vp, att, full, mixed_ref,
+    gate, up, down, normed, hid, gate_acc, up_acc,
     s0, s1, r0, r1, t0, t1, q0, q1, o0, o1, b0, b1, c0, c1, f0, f1,
-    wsem, ssem, rsem,
-):
-    e, x, g = lax.axis_index("ep"), lax.axis_index("rep"), lax.axis_index("groups")
-    rows, width = mixed_ref.shape
-    ff = gate.shape[1]
-    half = nx * ne
-    loads = [
-        pltpu.make_async_copy(gate_hbm, gate, wsem.at[0]),
-        pltpu.make_async_copy(up_hbm, up, wsem.at[1]),
-        pltpu.make_async_copy(down_hbm, down, wsem.at[2]),
-    ]
-    for load in loads:
-        load.start()
-    barrier = pltpu.get_barrier_semaphore()
-    for i in range(1, nx):
-        peer = (g, e, lax.rem(x + i, nx))
-        pl.semaphore_signal(barrier, inc=1, device_id=peer, device_id_type=MESH)
-    for i in range(1, ne):
-        peer = (g, lax.rem(e + i, ne), x)
-        pl.semaphore_signal(barrier, inc=1, device_id=peer, device_id_type=MESH)
-
-    widened = mixed_ref[...].astype(F32)
-    scale = lax.rsqrt(jnp.mean(widened * widened, axis=-1, keepdims=True) + EPS)
-    normed[...] = (widened * scale * gain_ref[...]).astype(BF16)
-
-    row, col = row_ref[...], col_ref[...]
-    first = lax.broadcasted_iota(jnp.int32, (rows, rows), 0)
-    second = lax.broadcasted_iota(jnp.int32, (rows, rows), 1)
-    earlier = jnp.where((row == col) & (first < second), 1, 0)
-    rank = jnp.sum(earlier, axis=0, keepdims=True)
-    slot = lax.broadcasted_iota(jnp.int32, (half, rows), 0)
-    turned = lax.rem(slot, ne) * nx + slot // ne
-    pick0 = one_hot((turned == row) & (rank == 0))
-    pick1 = one_hot((slot == row) & (rank == 1))
-
-    here = lax.broadcasted_iota(jnp.int32, (half, half), 0)
-    there = lax.broadcasted_iota(jnp.int32, (half, half), 1)
-    to_ex = one_hot(there == lax.rem(here, nx) * ne + here // nx)
-    to_xe = one_hot(there == lax.rem(here, ne) * nx + here // ne)
-
-    tile = 512
-
-    def over_columns(body):
-        def step(i, carry):
-            body(pl.ds(pl.multiple_of(i * tile, tile), tile))
-            return carry
-
-        lax.fori_loop(0, width // tile, step, 0)
-
-    def put(ref, cols, value):
-        ref[:, :, cols] = value.reshape(ref.shape[0], ref.shape[1], tile).astype(BF16)
-
-    def get(ref, cols):
-        return ref[:, :, cols].astype(F32).reshape(half, tile).astype(BF16)
-
-    def send_x(src, dst, k):
-        for i in range(1, nx):
-            to = lax.rem(x + i, nx)
-            pltpu.make_async_remote_copy(
-                src.at[to], dst.at[x], ssem.at[k], rsem.at[k],
-                device_id=(g, e, to), device_id_type=MESH,
-            ).start()
-
-    def send_e(src, dst, k):
-        for i in range(1, ne):
-            to = lax.rem(e + i, ne)
-            pltpu.make_async_remote_copy(
-                src.at[to], dst.at[e], ssem.at[k], rsem.at[k],
-                device_id=(g, to, x), device_id_type=MESH,
-            ).start()
-
-    def arrive(src, dst, k):
-        n = dst.shape[0] - 1
-        pltpu.make_async_copy(src.at[pl.ds(0, n)], dst.at[pl.ds(0, n)], ssem.at[k]).wait()
-        pltpu.make_async_copy(src.at[pl.ds(0, n)], dst.at[pl.ds(0, n)], rsem.at[k]).wait()
-
-    def scatter(cols):
-        put(s0, cols, dot(pick0, normed[:, cols]))
-        put(s1, cols, dot(pick1, normed[:, cols]))
-
-    over_columns(scatter)
-    pl.semaphore_wait(barrier, nx + ne - 2)
-    send_x(s0, r0, 0)
-    send_e(s1, r1, 1)
-    r0[x] = s0[x]
-    r1[e] = s1[e]
-    arrive(s0, r0, 0)
-    over_columns(lambda cols: put(t0, cols, dot(to_ex, get(r0, cols))))
-    send_e(t0, q0, 2)
-    q0[e] = t0[e]
-    arrive(s1, r1, 1)
-    over_columns(lambda cols: put(t1, cols, dot(to_xe, get(r1, cols))))
-    send_x(t1, q1, 3)
-    q1[x] = t1[x]
-
-    for load in loads:
-        load.wait()
-    arrive(t0, q0, 2)
-    arrive(t1, q1, 3)
-
-    def collect(cols):
-        xin[pl.ds(0, half), cols] = get(q0, cols)
-        xin[pl.ds(half, half), cols] = get(q1, cols)
-
-    over_columns(collect)
-    ftile = 256
-
-    def inner(i, carry):
-        cols = pl.ds(pl.multiple_of(i * ftile, ftile), ftile)
-        gate_proj = dot(xin[...], gate[:, cols])
-        up_proj = dot(xin[...], up[:, cols])
-        hid[:, cols] = (jax.nn.silu(gate_proj) * up_proj).astype(BF16)
-        return carry
-
-    lax.fori_loop(0, ff // ftile, inner, 0)
-
-    def outer(cols):
-        put(o0, cols, dot(hid[pl.ds(0, half), :], down[:, cols]))
-        put(o1, cols, dot(hid[pl.ds(half, half), :], down[:, cols]))
-
-    over_columns(outer)
-    send_e(o0, b0, 4)
-    send_x(o1, b1, 5)
-    b0[e] = o0[e]
-    b1[x] = o1[x]
-    arrive(o0, b0, 4)
-    over_columns(lambda cols: put(c0, cols, dot(to_xe, get(b0, cols))))
-    send_x(c0, f0, 6)
-    f0[x] = c0[x]
-    arrive(o1, b1, 5)
-    over_columns(lambda cols: put(c1, cols, dot(to_ex, get(b1, cols))))
-    send_e(c1, f1, 7)
-    f1[e] = c1[e]
-    arrive(c0, f0, 6)
-    arrive(c1, f1, 7)
-
-    def combine(cols):
-        moe = dot_t(pick0, get(f0, cols)) + dot_t(pick1, get(f1, cols))
-        out_ref[:, cols] = (mixed_ref[:, cols].astype(F32) + moe).astype(BF16)
-
-    over_columns(combine)
-
-
-def moe(mixed, gain, row, col, gate_weight, up_weight, down_weight):
-    nx, ne = lax.axis_size("rep"), lax.axis_size("ep")
-    rows, width = mixed.shape
-    ff = gate_weight.shape[2]
-    half = nx * ne
-    xe = pltpu.VMEM((nx, ne, width), BF16)
-    ex = pltpu.VMEM((ne, nx, width), BF16)
-    vmem, any_ = pl.BlockSpec(memory_space=pltpu.VMEM), pl.BlockSpec(memory_space=pl.ANY)
-    return pl.pallas_call(
-        functools.partial(moe_kernel, nx, ne),
-        out_shape=jax.ShapeDtypeStruct((rows, width), BF16),
-        in_specs=[vmem] * 4 + [any_] * 3,
-        out_specs=vmem,
-        scratch_shapes=[
-            pltpu.VMEM((width, ff), BF16), pltpu.VMEM((width, ff), BF16), pltpu.VMEM((ff, width), BF16),
-            pltpu.VMEM((rows, width), BF16), pltpu.VMEM((2 * half, width), BF16), pltpu.VMEM((2 * half, ff), BF16),
-            xe, ex, xe, ex, ex, xe, ex, xe, ex, xe, ex, xe, xe, ex, xe, ex,
-            pltpu.SemaphoreType.DMA((3,)), pltpu.SemaphoreType.DMA((8,)), pltpu.SemaphoreType.DMA((8,)),
-        ],
-        compiler_params=pltpu.CompilerParams(
-            collective_id=1, has_side_effects=True, vmem_limit_bytes=48 << 20
-        ),
-        name="moe",
-    )(
-        mixed, gain.reshape(1, width), row, col,
-        gate_weight[0], up_weight[0], down_weight[0],
-    )
-
-
-SHARED_ROWS = 1280
-
-
-def front_kernel(
-    nx, ne, prompt_ref, hidden_ref, query_ref, gain_ref, lengths_ref, ids_ref, idcol_ref,
-    kvw_hbm, ow_hbm, table_hbm, mixed_ref, col_ref, row_ref,
-    kvw, ow, table, picked, hn, pn, qf, qt, skv, dkv, spk, pkv, pf, kp, vp, att, full,
-    lsem, ring_send, ring_recv, dd_send, dd_recv, xs, xr,
+    lsem, wsem, ring_send, ring_recv, dd_send, dd_recv, xs, xr, msend, mrecv,
 ):
     e, x, g = lax.axis_index("ep"), lax.axis_index("rep"), lax.axis_index("groups")
     ny = ne // 2
     y, c = e // 2, lax.rem(e, 2)
-    rows, width = hidden_ref.shape
+    rows, width = hidden_hbm.shape
     shared = SHARED_ROWS
     piece = shared // ne
     sub = (width - shared) // 4
     orow = ow.shape[1] // ne
     half = ow.shape[2] // 2
-    plen = prompt_ref.shape[0] // GROUP_PROMPTS
+    plen = prompt_hbm.shape[0] // GROUP_PROMPTS
     own_prompt = e // (ne // GROUP_PROMPTS)
     seqs = 16
 
@@ -248,9 +76,19 @@
         pltpu.make_async_copy(
             ow_hbm.at[piece_rows(e, orow, orow)], ow.at[x, piece_rows(e, orow, orow)], lsem.at[2]
         ),
-        pltpu.make_async_copy(table_hbm, table, lsem.at[3]),
     ]
-    for load in loads:
+    late = [
+        pltpu.make_async_copy(hidden_hbm, hidden_ref, lsem.at[3]),
+        pltpu.make_async_copy(prompt_hbm, prompt_ref, lsem.at[4]),
+        pltpu.make_async_copy(query_hbm, query_ref, lsem.at[5]),
+        pltpu.make_async_copy(table_hbm, table, lsem.at[6]),
+    ]
+    weights = [
+        pltpu.make_async_copy(gate_hbm, gate, wsem.at[0]),
+        pltpu.make_async_copy(up_hbm, up, wsem.at[1]),
+        pltpu.make_async_copy(down_hbm, down, wsem.at[2]),
+    ]
+    for load in loads + late:
         load.start()
 
     sibling = (g, 2 * y + 1 - c, x)
@@ -264,9 +102,9 @@
     barrier = pltpu.get_barrier_semaphore()
     for i in range(1, nx):
         pl.semaphore_signal(barrier, inc=1, device_id=at_x(i), device_id_type=MESH)
-    for i in range(1, ny):
-        pl.semaphore_signal(barrier, inc=1, device_id=at_y(i), device_id_type=MESH)
-    pl.semaphore_signal(barrier, inc=1, device_id=sibling, device_id_type=MESH)
+    for i in range(1, ne):
+        peer = (g, lax.rem(e + i, ne), x)
+        pl.semaphore_signal(barrier, inc=1, device_id=peer, device_id_type=MESH)
 
     class Ring:
         def __init__(self, number, along, sign, hops, chunk, total, mate):
@@ -351,9 +189,10 @@
         scale = lax.rsqrt(jnp.mean(widened * widened, axis=-1, keepdims=True) + EPS)
         out[...] = (widened * scale * gain_ref[...]).astype(BF16)
 
-    for load in loads:
-        load.wait()
-    pl.semaphore_wait(barrier, nx + ny - 1)
+    with jax.named_scope("enter"):
+        for load in loads:
+            load.wait()
+        pl.semaphore_wait(barrier, nx + ne - 2)
 
     own_piece = piece_rows(e, piece, piece)
     for i in range(1, nx):
@@ -365,6 +204,8 @@
         ring.go(0)
     for ring in ow_x:
         ring.go(0)
+    for load in late:
+        load.wait()
     normalised(hidden_ref, hn)
     ref = kvw.at[pl.ds(0, nx - 1), pl.ds(0, piece)]
     pltpu.make_async_copy(ref, ref, xs.at[0]).wait()
@@ -375,12 +216,15 @@
         to_mate(kvw.at[pl.ds(4 * s, 4), own_piece], 1)
 
     for h in range(1, 5):
-        for ring in kv_x:
-            ring.event(h)
-        for ring in kv_y:
-            ring.event(h)
-        for ring in ow_x:
-            ring.event(h)
+        with jax.named_scope("kv_x"):
+            for ring in kv_x:
+                ring.event(h)
+        with jax.named_scope("kv_y"):
+            for ring in kv_y:
+                ring.event(h)
+        with jax.named_scope("ow_x"):
+            for ring in ow_x:
+                ring.event(h)
         if h == 1:
             normalised(prompt_ref, pn)
             for k in range(2):
@@ -397,13 +241,8 @@
                 return carry
 
             lax.fori_loop(0, rows, look, 0)
-            lane = lax.broadcasted_iota(jnp.int32, (rows, 128), 1)
-            line = lax.broadcasted_iota(jnp.int32, (rows, 128), 0)
-            chosen = jnp.sum(
-                jnp.where(lane == lax.rem(idcol_ref[...], 128), picked[...], 0), axis=1, keepdims=True
-            )
-            col_ref[...] = chosen
-            row_ref[...] = jnp.sum(jnp.where(lane == line, chosen, 0), axis=0, keepdims=True)
+            for weight in weights:
+                weight.start()
     mate_done(kvw.at[pl.ds(0, nx - 1), pl.ds(0, 2 * sub)], 0)
     mate_done(kvw.at[pl.ds(0, nx), pl.ds(0, ny * piece)], 1)
 
@@ -529,31 +368,157 @@
         return carry
 
     lax.fori_loop(0, width // tile, project, 0)
+    lane = lax.broadcasted_iota(jnp.int32, (rows, rows), 1)
+    line = lax.broadcasted_iota(jnp.int32, (rows, rows), 0)
+    idcol = jnp.sum(jnp.where(lane == line, idrow_ref[...], 0), axis=1, keepdims=True)
+    col = jnp.sum(jnp.where(lane == lax.rem(idcol, 128), picked[...], 0), axis=1, keepdims=True)
+    row = jnp.sum(jnp.where(lane == line, col, 0), axis=0, keepdims=True)
+    earlier = jnp.where((row == col) & (line < lane), 1, 0)
+    rank = jnp.sum(earlier, axis=0, keepdims=True)
+    cells = nx * ne
+    slot = lax.broadcasted_iota(jnp.int32, (cells, rows), 0)
+    swapped = lax.rem(slot, ne) * nx + slot // ne
+    pick0 = one_hot((swapped == row) & (rank == 0))
+    pick1 = one_hot((slot == row) & (rank == 1))
+    here = lax.broadcasted_iota(jnp.int32, (cells, cells), 0)
+    there = lax.broadcasted_iota(jnp.int32, (cells, cells), 1)
+    to_ex = one_hot(there == lax.rem(here, nx) * ne + here // nx)
+    to_xe = one_hot(there == lax.rem(here, ne) * nx + here // ne)
+
+    with jax.named_scope("moe_norm"):
+        widened = mixed_ref[...].astype(F32)
+        scale = lax.rsqrt(jnp.mean(widened * widened, axis=-1, keepdims=True) + EPS)
+        normed[...] = (widened * scale * moe_gain_ref[...]).astype(BF16)
+
+    part = width // CHUNKS
+    tile = 512
+
+    def tiles(chunk, body):
+        def step(i, carry):
+            body(pl.ds(pl.multiple_of(chunk * part + i * tile, tile), tile))
+            return carry
+
+        lax.fori_loop(0, part // tile, step, 0)
+
+    def put(ref, cols, value):
+        ref[:, :, cols] = value.reshape(ref.shape[0], ref.shape[1], tile).astype(BF16)
+
+    def get(ref, cols):
+        return ref[:, :, cols].astype(F32).reshape(cells, tile).astype(BF16)
+
+    def send(src, dst, k, chunk):
+        n = dst.shape[0]
+        me = x if n == nx else e
+        cols = pl.ds(chunk * part, part)
+        for i in range(1, n):
+            to = lax.rem(me + i, n)
+            pltpu.make_async_remote_copy(
+                src.at[to, :, cols], dst.at[me, :, cols], msend.at[k, chunk], mrecv.at[k, chunk],
+                device_id=(g, e, to) if n == nx else (g, to, x), device_id_type=MESH,
+            ).start()
+        dst[me, :, cols] = src[me, :, cols]
+
+    def arrive(dst, k, chunk):
+        ref = dst.at[pl.ds(0, dst.shape[0] - 1), :, pl.ds(chunk * part, part)]
+        pltpu.make_async_copy(ref, ref, msend.at[k, chunk]).wait()
+        pltpu.make_async_copy(ref, ref, mrecv.at[k, chunk]).wait()
+
+    def two_phases(base, a0, m0, n0, d0, a1, m1, n1, d1, order0, order1, fill):
+        for chunk in range(CHUNKS):
+            with jax.named_scope("fill"):
+                fill(chunk)
+            send(a0, m0, base, chunk)
+            send(a1, m1, base + 1, chunk)
+        for chunk in range(CHUNKS):
+            with jax.named_scope("wait_first"):
+                arrive(m0, base, chunk)
+            with jax.named_scope("permute"):
+                tiles(chunk, lambda cols: put(n0, cols, dot(order0, get(m0, cols))))
+            send(n0, d0, base + 2, chunk)
+            with jax.named_scope("wait_first"):
+                arrive(m1, base + 1, chunk)
+            with jax.named_scope("permute"):
+                tiles(chunk, lambda cols: put(n1, cols, dot(order1, get(m1, cols))))
+            send(n1, d1, base + 3, chunk)
+
+    def scatter(chunk):
+        def body(cols):
+            put(s0, cols, dot(pick0, normed[:, cols]))
+            put(s1, cols, dot(pick1, normed[:, cols]))
+
+        tiles(chunk, body)
+
+    two_phases(0, s0, r0, t0, q0, s1, r1, t1, q1, to_ex, to_xe, scatter)
+    with jax.named_scope("weights"):
+        for weight in weights:
+            weight.wait()
+
+    ff = gate.shape[1]
+    ftile = 256
+    for chunk in range(CHUNKS):
+        with jax.named_scope("wait_second"):
+            arrive(q0, 2, chunk)
+            arrive(q1, 3, chunk)
+        with jax.named_scope("inner"):
+            cols = pl.ds(chunk * part, part)
+            tokens = jnp.concatenate(
+                [q[:, :, cols].astype(F32).reshape(cells, part).astype(BF16) for q in (q0, q1)], axis=0
+            )
+            if chunk == 0:
+                gate_acc[...] = dot(tokens, gate[cols, :])
+                up_acc[...] = dot(tokens, up[cols, :])
+            else:
+                gate_acc[...] += dot(tokens, gate[cols, :])
+                up_acc[...] += dot(tokens, up[cols, :])
+    with jax.named_scope("silu"):
+        hid[...] = (jax.nn.silu(gate_acc[...]) * up_acc[...]).astype(BF16)
+
+    def outer(chunk):
+        def body(cols):
+            put(o0, cols, dot(hid[pl.ds(0, cells), :], down[:, cols]))
+            put(o1, cols, dot(hid[pl.ds(cells, cells), :], down[:, cols]))
+
+        tiles(chunk, body)
+
+    two_phases(4, o0, b0, c0, f0, o1, b1, c1, f1, to_xe, to_ex, outer)
+    for chunk in range(CHUNKS):
+        with jax.named_scope("wait_second"):
+            arrive(f0, 6, chunk)
+            arrive(f1, 7, chunk)
+
+        def combine(cols):
+            moe = dot_t(pick0, get(f0, cols)) + dot_t(pick1, get(f1, cols))
+            out_ref[:, cols] = (mixed_ref[:, cols].astype(F32) + moe).astype(BF16)
+
+        with jax.named_scope("combine"):
+            tiles(chunk, combine)
     for ring in kv_x + kv_y + ow_x + ow_y:
         ring.finish()
 
 
-def front(prompt, hidden, queries, gain, lengths, ids, kvw, ow, expert_table):
+def layer(prompt, hidden, queries, gain, moe_gain, lengths, ids, kvw, ow, expert_table, gate, up, down):
     nx, ne = lax.axis_size("rep"), lax.axis_size("ep")
     rows, width = hidden.shape
     count = prompt.shape[0]
     plen = count // GROUP_PROMPTS
     keys = plen * ne
+    ff = gate.shape[1]
     vmem, any_ = pl.BlockSpec(memory_space=pltpu.VMEM), pl.BlockSpec(memory_space=pl.ANY)
     smem = pl.BlockSpec(memory_space=pltpu.SMEM)
     cols = queries.shape[1]
     table = expert_table.reshape(-1, 128)
     sem = pltpu.SemaphoreType.DMA
+    xe = pltpu.VMEM((nx, ne, width), BF16)
+    ex = pltpu.VMEM((ne, nx, width), BF16)
     return pl.pallas_call(
-        functools.partial(front_kernel, nx, ne),
-        out_shape=(
-            jax.ShapeDtypeStruct((rows, width), BF16),
-            jax.ShapeDtypeStruct((rows, 1), jnp.int32),
-            jax.ShapeDtypeStruct((1, rows), jnp.int32),
-        ),
-        in_specs=[vmem] * 4 + [smem] * 2 + [vmem] + [any_] * 3,
-        out_specs=(vmem, vmem, vmem),
+        functools.partial(layer_kernel, nx, ne),
+        out_shape=jax.ShapeDtypeStruct((rows, width), BF16),
+        in_specs=[any_] * 3 + [vmem] * 2 + [smem] * 2 + [vmem] + [any_] * 6,
+        out_specs=vmem,
         scratch_shapes=[
+            pltpu.VMEM(prompt.shape, BF16),
+            pltpu.VMEM(hidden.shape, BF16),
+            pltpu.VMEM(queries.shape, BF16),
             pltpu.VMEM((nx,) + kvw.shape, BF16),
             pltpu.VMEM((nx,) + ow.shape, BF16),
             pltpu.VMEM(table.shape, jnp.int32),
@@ -571,15 +536,21 @@
             pltpu.VMEM((keys, HEAD_DIM), BF16),
             pltpu.VMEM((nx, rows, cols), BF16),
             pltpu.VMEM((nx, rows, cols), BF16),
-            sem((4,)), sem((16,)), sem((16, 4)), sem((4,)), sem((4,)), sem((4,)), sem((4,)),
+            pltpu.VMEM((rows, width), BF16),
+            pltpu.VMEM(gate.shape, BF16), pltpu.VMEM(up.shape, BF16), pltpu.VMEM(down.shape, BF16),
+            pltpu.VMEM((rows, width), BF16), pltpu.VMEM((2 * nx * ne, ff), BF16),
+            pltpu.VMEM((2 * nx * ne, ff), F32), pltpu.VMEM((2 * nx * ne, ff), F32),
+            xe, ex, xe, ex, ex, xe, ex, xe, ex, xe, ex, xe, xe, ex, xe, ex,
+            sem((7,)), sem((3,)), sem((16,)), sem((16, 4)), sem((4,)), sem((4,)), sem((4,)), sem((4,)),
+            sem((8, CHUNKS)), sem((8, CHUNKS)),
         ],
         compiler_params=pltpu.CompilerParams(
-            collective_id=0, has_side_effects=True, vmem_limit_bytes=48 << 20
+            collective_id=0, has_side_effects=True, vmem_limit_bytes=67043328
         ),
-        name="front",
+        name="layer",
     )(
-        prompt, hidden, queries, gain.reshape(1, width), lengths, ids.reshape(rows), ids.reshape(rows, 1),
-        kvw, ow, table,
+        prompt, hidden, queries, gain.reshape(1, width), moe_gain.reshape(1, width), lengths,
+        ids.reshape(rows), ids.reshape(1, rows), kvw, ow, table, gate, up, down,
     )
 
 
@@ -598,20 +569,22 @@
     token_ids,
     prompt_lengths,
 ):
-    rows = decode_hidden.shape[0] * decode_hidden.shape[1]
     width = decode_hidden.shape[2]
-    mixed, col, row = front(
+    out = layer(
         prompt_hidden.reshape(-1, width),
-        decode_hidden.reshape(rows, width),
+        decode_hidden.reshape(-1, width),
         queries.reshape(-1, queries.shape[2]),
         attn_gain,
+        moe_gain,
         prompt_lengths,
         token_ids,
         key_value_weight,
         out_weight,
         expert_table,
-    )
-    out = moe(mixed, moe_gain, row, col, gate_weight, up_weight, down_weight)
+        gate_weight[0],
+        up_weight[0],
+        down_weight[0],
+    )
     return out.reshape(decode_hidden.shape)
 
 

time: 178 us -> 159 us (0.89)
  Pallas kernels: 168 us -> 157 us
  local copies, waits for them, and re-layouts: 10.2 us -> 1.88 us
    pallas_call x2 -> x1, Pallas kernels: 168 us -> 157 us  [layer(): pl.pallas_call(functools.partial(layer_kernel, nx, ne), out_shape=jax.Sha...]
    unnamed x24 -> x1, local copies, waits for them, and re-layouts: 10.2 us -> 1.88 us
where the time goes in v3:
time: 159 us
  Pallas kernels  157 us (99%)
  local copies, waits for them, and re-layouts  1.88 us (1%)
    pallas_call x1, Pallas kernels, layer(): pl.pallas_call(functools.partial(layer_kernel, nx, ne), out_shape=jax.Sha...  157 us

profile of v3, /device:TPU:513, one launch (start us, length us, event | category | flops | bytes accessed | tf_op | source)
XLA Modules:
  0.0 158.6 jit_solution(10786827892408872657)
XLA Ops:
  0.0 156.7 %layer.1 = bf16[128,2048]{1,0:T(8,128)(2,1)} custom-call(bf16[96,2048]{1,0:T(8,128)(2,1)} %bitcast.19, bf16[128,2048]{1,0:T(8,128)(2,1)} %bitcast.17, bf16[1024,256]{1,0:T(8,128)(2,1)} %bitcast.18, f32[1,2048]{1,0:T(1,128)} %bitcast.20, f32[1,2048]{1,0:T(1,128)} %bitcast.21, s32[4]{0:T(128)} %lengths_ref.1, s32[128]{0:T(128)} %bitcast.22, ...), custom_call_target="tpu_custom_call" | custom-call | tf_op jit(solution)/shard_map/layer/pallas_call | solution.py:513
  156.7 1.9 %copy.15 = bf16[128,1,2048]{2,0,1:T(8,128)(2,1)} copy(bf16[128,1,2048]{2,0,1:T(8,128)(2,1)} %bitcast.15) | data formatting | bytes 1048576

commit v4 on v3

--- a/solution.py
+++ b/solution.py
@@ -33,7 +33,9 @@
     return jnp.where(hit, 1.0, 0.0).astype(BF16)
 
 
-SHARED_ROWS = 1280
+SHARED_ROWS = 1024
+DIRECT = 512
+FAR = 4
 CHUNKS = 2
 
 
@@ -41,7 +43,7 @@
     nx, ne, prompt_hbm, hidden_hbm, query_hbm, gain_ref, moe_gain_ref, lengths_ref, ids_ref, idrow_ref,
     kvw_hbm, ow_hbm, table_hbm, gate_hbm, up_hbm, down_hbm, out_ref,
     prompt_ref, hidden_ref, query_ref,
-    kvw, ow, table, picked, hn, pn, qf, qt, skv, dkv, spk, pkv, pf, kp, vp, att, full, mixed_ref,
+    kvw, ow, table, picked, hn, pn, qf, qt, skv, dkv, spk, pkv, pf, kp, vp, att, full, mixed_ref, top_p, total_p, summed_p,
     gate, up, down, normed, hid, gate_acc, up_acc,
     s0, s1, r0, r1, t0, t1, q0, q1, o0, o1, b0, b1, c0, c1, f0, f1,
     lsem, wsem, ring_send, ring_recv, dd_send, dd_recv, xs, xr, msend, mrecv,
@@ -54,14 +56,15 @@
     piece = shared // ne
     sub = (width - shared) // 4
     orow = ow.shape[1] // ne
-    half = ow.shape[2] // 2
+    half = (width - DIRECT) // 2
+    lines = ow.shape[1] // 4
+    spread_cols = pl.ds(DIRECT, width - DIRECT)
     plen = prompt_hbm.shape[0] // GROUP_PROMPTS
     own_prompt = e // (ne // GROUP_PROMPTS)
     seqs = 16
 
     def sub_rows(core, s):
-        start = pl.multiple_of(shared + core * (2 * sub) + s * sub, 16)
-        return pl.ds(start, sub)
+        return pl.ds(pl.multiple_of(shared + core * (2 * sub) + s * sub, 16), sub)
 
     def piece_rows(k, size, unit):
         return pl.ds(pl.multiple_of(k * unit, 16), size)
@@ -74,8 +77,11 @@
             kvw_hbm.at[piece_rows(e, piece, piece)], kvw.at[x, piece_rows(e, piece, piece)], lsem.at[1]
         ),
         pltpu.make_async_copy(
-            ow_hbm.at[piece_rows(e, orow, orow)], ow.at[x, piece_rows(e, orow, orow)], lsem.at[2]
+            ow_hbm.at[piece_rows(e, orow, orow), spread_cols],
+            ow.at[FAR, piece_rows(e, orow, orow), spread_cols],
+            lsem.at[2],
         ),
+        pltpu.make_async_copy(ow_hbm.at[:, pl.ds(0, DIRECT)], ow.at[FAR, :, pl.ds(0, DIRECT)], lsem.at[7]),
     ]
     late = [
         pltpu.make_async_copy(hidden_hbm, hidden_ref, lsem.at[3]),
@@ -107,26 +113,30 @@
         pl.semaphore_signal(barrier, inc=1, device_id=peer, device_id_type=MESH)
 
     class Ring:
-        def __init__(self, number, along, sign, hops, chunk, total, mate):
-            self.along, self.sign, self.hops, self.chunk = along, sign, hops, chunk
+        def __init__(self, number, along, sign, hops, place, total, mate):
+            self.along, self.sign, self.hops, self.place = along, sign, hops, place
             self.number, self.total, self.mate = number, total, mate
 
         def origin(self, h):
             me, n = (x, nx) if self.along == "x" else (y, ny)
             return lax.rem(me - self.sign * h + n, n)
 
+        def at(self, h):
+            return self.place(self.origin(h), (FAR - self.sign * h) % (2 * FAR))
+
         def go(self, h):
-            ref = self.chunk(self.origin(h))
+            ref = self.at(h)
+            there = self.place(self.origin(h), (FAR - self.sign * (h + 1)) % (2 * FAR))
             to = at_x(self.sign) if self.along == "x" else at_y(self.sign)
             pltpu.make_async_remote_copy(
-                ref, ref, ring_send.at[self.number], ring_recv.at[self.number, h],
+                ref, there, ring_send.at[self.number], ring_recv.at[self.number, h],
                 device_id=to, device_id_type=MESH,
             ).start()
 
         def event(self, h):
             if h > self.hops:
                 return
-            ref = self.chunk(self.origin(h))
+            ref = self.at(h)
             pltpu.make_async_copy(ref, ref, ring_recv.at[self.number, h - 1]).wait()
             if h < self.hops:
                 self.go(h)
@@ -146,43 +156,73 @@
         pltpu.make_async_copy(ref, ref, dd_send.at[k]).wait()
         pltpu.make_async_copy(ref, ref, dd_recv.at[k]).wait()
 
-    def rings(base, along, chunk, total, mate):
-        made = []
-        for s in range(2):
-            for sign in (1, -1):
-                hops = 4 if (s == 0) == (sign == 1) else 3
-                made.append(
-                    Ring(
-                        base + len(made), along, sign, hops,
-                        functools.partial(chunk, s), functools.partial(total, s), mate,
-                    )
-                )
-        return made
-
-    kv_x = rings(
-        0, "x",
-        lambda s, k: kvw.at[k, sub_rows(c, s)],
-        lambda s, n: kvw.at[pl.ds(0, n), sub_rows(0, s)],
-        0,
-    )
-    kv_y = rings(
-        4, "y",
-        lambda s, k: kvw.at[pl.ds(4 * s, 4), piece_rows(2 * k + c, piece, piece)],
-        lambda s, n: kvw.at[pl.ds(4 * s, 4), pl.ds(0, n * piece)],
-        1,
-    )
-    ow_x = rings(
-        8, "x",
-        lambda s, k: ow.at[k, piece_rows(e, orow, orow), pl.ds(s * half, half)],
-        lambda s, n: ow.at[pl.ds(0, n), pl.ds(0, orow), pl.ds(s * half, half)],
-        None,
-    )
-    ow_y = rings(
-        12, "y",
-        lambda s, k: ow.at[pl.ds(4 * s, 4), piece_rows(2 * k + c, orow, orow)],
-        lambda s, n: ow.at[pl.ds(4 * s, 4), pl.ds(0, n * orow)],
-        2,
-    )
+    def pair(base, along, more, place, total, mate):
+        return [
+            Ring(base, along, 1, 4 if more else 3, place, total, mate),
+            Ring(base + 1, along, -1, 3 if more else 4, place, total, mate),
+        ]
+
+    def kv_pair(base, s):
+        return pair(
+            base, "x", s == 0,
+            lambda j, i: kvw.at[j, sub_rows(c, s)],
+            lambda n: kvw.at[pl.ds(0, n), pl.ds(0, sub)],
+            0,
+        )
+
+    def kv_spread(base, s):
+        slices = pl.ds(4 * s, 4)
+        return pair(
+            base, "y", s == 0,
+            lambda k, i: kvw.at[slices, piece_rows(2 * k + c, piece, piece)],
+            lambda n: kvw.at[slices, pl.ds(0, n * piece)],
+            3,
+        )
+
+    def spread_pair(base, s):
+        return pair(
+            base, "x", s == 0,
+            lambda j, i: ow.at[i, piece_rows(e, orow, orow), pl.ds(DIRECT + s * half, half)],
+            lambda n: ow.at[pl.ds(0, n), pl.ds(0, orow), pl.ds(0, half)],
+            None,
+        )
+
+    def ow_pair(base, more, first, n_slices):
+        slices = pl.ds(first, n_slices)
+        return pair(
+            base, "y", more,
+            lambda k, i: ow.at[
+                slices, piece_rows(2 * k + c, orow, orow), spread_cols
+            ],
+            lambda n: ow.at[slices, pl.ds(0, n * orow), spread_cols],
+            1,
+        )
+
+    def direct_pair(base, s):
+        return pair(
+            base, "x", s == 0,
+            lambda j, i: ow.at[
+                i, pl.ds(pl.multiple_of(c * (2 * lines) + s * lines, 16), lines), pl.ds(0, DIRECT)
+            ],
+            lambda n: ow.at[pl.ds(0, n), pl.ds(0, lines), pl.ds(0, DIRECT)],
+            4,
+        )
+
+    straight = direct_pair(18, 0) + direct_pair(20, 1)
+    kv_x = kv_pair(0, 0) + kv_pair(2, 1)
+    kv_y = kv_spread(14, 0) + kv_spread(16, 1)
+    ow_x = spread_pair(4, 0) + spread_pair(6, 1)
+    near = ow_pair(8, True, FAR - 1, 3)
+    rest = ow_pair(10, False, 0, FAR - 1) + ow_pair(12, True, FAR + 2, nx - FAR - 2)
+
+    def events(rings, h):
+        for ring in rings:
+            ring.event(h)
+
+    def begin(rings, slices):
+        for ring in rings:
+            ring.go(0)
+        to_mate(ow.at[slices, piece_rows(e, orow, orow), spread_cols], 1)
 
     def normalised(ref, out):
         widened = ref[...].astype(F32)
@@ -202,49 +242,50 @@
         ).start()
     for ring in kv_x:
         ring.go(0)
-    for ring in ow_x:
-        ring.go(0)
     for load in late:
         load.wait()
     normalised(hidden_ref, hn)
-    ref = kvw.at[pl.ds(0, nx - 1), pl.ds(0, piece)]
-    pltpu.make_async_copy(ref, ref, xs.at[0]).wait()
-    pltpu.make_async_copy(ref, ref, xr.at[0]).wait()
+    with jax.named_scope("spread_wait"):
+        ref = kvw.at[pl.ds(0, nx - 1), pl.ds(0, piece)]
+        pltpu.make_async_copy(ref, ref, xs.at[0]).wait()
+        pltpu.make_async_copy(ref, ref, xr.at[0]).wait()
     for ring in kv_y:
         ring.go(0)
+    for ring in ow_x:
+        ring.go(0)
     for s in range(2):
-        to_mate(kvw.at[pl.ds(4 * s, 4), own_piece], 1)
-
+        to_mate(kvw.at[pl.ds(4 * s, 4), own_piece], 3)
     for h in range(1, 5):
-        with jax.named_scope("kv_x"):
-            for ring in kv_x:
-                ring.event(h)
-        with jax.named_scope("kv_y"):
-            for ring in kv_y:
-                ring.event(h)
-        with jax.named_scope("ow_x"):
-            for ring in ow_x:
-                ring.event(h)
+        with jax.named_scope(f"kv_x#h={h}"):
+            events(kv_x, h)
+        if h == 4:
+            with jax.named_scope("ow_x#h=4"):
+                events(ow_x, 4)
+            begin(rest, pl.ds(0, FAR - 1))
+            to_mate(ow.at[pl.ds(FAR + 2, nx - FAR - 2), piece_rows(e, orow, orow), spread_cols], 1)
+        with jax.named_scope(f"kv_y#h={h}"):
+            events(kv_y, h)
+        if h == 3:
+            begin(near, pl.ds(FAR - 1, 3))
+            for ring in straight:
+                ring.go(0)
+        if h < 4:
+            with jax.named_scope(f"ow_x#h={h}"):
+                events(ow_x, h)
         if h == 1:
             normalised(prompt_ref, pn)
             for k in range(2):
                 qf[k] = query_ref[:, pl.ds(k * HEAD_DIM, HEAD_DIM)].astype(F32)
+            for weight in weights:
+                weight.start()
         if h == 2:
             for t in range(nx):
                 for k in range(2):
                     cols = pl.ds(k * HEAD_DIM, HEAD_DIM)
                     qt[t, :, cols] = qf[k, pl.ds(t, rows, stride=nx), :].astype(BF16)
-        if h == 3:
-            def look(i, carry):
-                at = lax.div(ids_ref[i], 128)
-                picked[pl.ds(i, 1), :] = table[pl.ds(at, 1), :]
-                return carry
-
-            lax.fori_loop(0, rows, look, 0)
-            for weight in weights:
-                weight.start()
-    mate_done(kvw.at[pl.ds(0, nx - 1), pl.ds(0, 2 * sub)], 0)
-    mate_done(kvw.at[pl.ds(0, nx), pl.ds(0, ny * piece)], 1)
+    with jax.named_scope("kv_mate"):
+        mate_done(kvw.at[pl.ds(0, nx - 1), pl.ds(0, 2 * sub)], 0)
+        mate_done(kvw.at[pl.ds(0, nx), pl.ds(0, ny * piece)], 3)
 
     length = lengths_ref[own_prompt]
     half_dim = HEAD_DIM // 2
@@ -261,22 +302,35 @@
 
     cosine, sine = turns(8, jnp.full((8, HEAD_DIM), length + x, jnp.int32))
     cosine, sine = cosine[0:1], sine[0:1]
-    for head in range(KEY_VALUE_HEADS):
+    def own_kv(head):
         skv[head, 0] = turned(dot(hn[...], kvw[2 * head]), cosine, sine).astype(BF16)
         skv[head, 1] = dot(hn[...], kvw[2 * head + 1]).astype(BF16)
-    for i in range(1, nx):
-        to = lax.rem(x + i, nx)
+
+    def send_kv(head, to):
         pltpu.make_async_remote_copy(
-            skv.at[to // 2], dkv.at[x], xs.at[1], xr.at[1], device_id=(g, e, to), device_id_type=MESH
+            skv.at[head], dkv.at[x], xs.at[1], xr.at[1], device_id=(g, e, to), device_id_type=MESH
         ).start()
+
+    with jax.named_scope("straight#h=1"):
+        events(straight, 1)
+    with jax.named_scope("own_kv"):
+        for i in (2, 1, 3, 0):
+            head = lax.rem(x // 2 + i, KEY_VALUE_HEADS)
+            own_kv(head)
+            if i:
+                send_kv(head, 2 * head)
+                send_kv(head, 2 * head + 1)
+            else:
+                send_kv(head, x + 1 - 2 * lax.rem(x, 2))
     dkv[x] = skv[x // 2]
 
     count = GROUP_PROMPTS * plen
     line = lax.broadcasted_iota(jnp.int32, (count, HEAD_DIM), 0)
     pcos, psin = turns(count, e * plen + lax.rem(line, plen))
     head = x // 2
-    pkey = turned(dot(pn[...], kvw[2 * head]), pcos, psin)
-    pval = dot(pn[...], kvw[2 * head + 1])
+    with jax.named_scope("prompt_kv"):
+        pkey = turned(dot(pn[...], kvw[2 * head]), pcos, psin)
+        pval = dot(pn[...], kvw[2 * head + 1])
     spk[:, 0] = pkey.reshape(GROUP_PROMPTS, plen, HEAD_DIM).astype(BF16)
     spk[:, 1] = pval.reshape(GROUP_PROMPTS, plen, HEAD_DIM).astype(BF16)
     per = ny // GROUP_PROMPTS
@@ -287,29 +341,28 @@
             device_id=(g, 2 * to + c, x), device_id_type=MESH,
         ).start()
     pkv[c, y] = spk[y // per]
-    for ring in ow_y:
-        ring.go(0)
-    for s in range(2):
-        to_mate(ow.at[pl.ds(4 * s, 4), piece_rows(e, orow, orow)], 2)
-
-    ref = pkv.at[0, pl.ds(0, ny - 1)]
-    pltpu.make_async_copy(ref, ref, xs.at[2]).wait()
-    pltpu.make_async_copy(ref, ref, xr.at[2]).wait()
-    to_mate(pkv.at[c], 3)
-    mate_done(pkv.at[0], 3)
+    with jax.named_scope("near#h=1"):
+        events(near, 1)
+
+    def look(i, carry):
+        at = lax.div(ids_ref[i], 128)
+        picked[pl.ds(i, 1), :] = table[pl.ds(at, 1), :]
+        return carry
+
+    with jax.named_scope("look"):
+        lax.fori_loop(0, rows, look, 0)
+    with jax.named_scope("prompt_wait"):
+        ref = pkv.at[0, pl.ds(0, ny - 1)]
+        pltpu.make_async_copy(ref, ref, xs.at[2]).wait()
+        pltpu.make_async_copy(ref, ref, xr.at[2]).wait()
+        to_mate(pkv.at[c], 2)
+        mate_done(pkv.at[0], 2)
     for k in range(2):
         for core in range(2):
             for row in range(ny):
                 start = (2 * row + core) * plen
                 pf[pl.ds(start, plen), :] = pkv[core, row, k].astype(F32)
         (kp if k == 0 else vp)[...] = pf[...].astype(BF16)
-
-    for ring in ow_y:
-        ring.event(1)
-
-    ref = dkv.at[pl.ds(0, nx - 1)]
-    pltpu.make_async_copy(ref, ref, xs.at[1]).wait()
-    pltpu.make_async_copy(ref, ref, xr.at[1]).wait()
 
     keys = kp.shape[0]
     block = 2 * nx * seqs
@@ -322,19 +375,34 @@
     def nt(a, b):
         return lax.dot_general(a, b, (((1,), (1,)), ((), ())), preferred_element_type=F32)
 
+    def asked(pick):
+        return jnp.concatenate(
+            [qt[:, pick, pl.ds(h * HEAD_DIM, HEAD_DIM)].reshape(nx * seqs, HEAD_DIM) for h in range(2)], axis=0
+        )
+
+    def twice(body, i, carry):
+        return body(2 * i + 1, body(2 * i, carry))
+
+    def attend_prompt(j, carry):
+        pick = pl.ds(pl.multiple_of(j * seqs, seqs), seqs)
+        scores = jnp.where(valid, nt(asked(pick), kp[...]) * scale, -1e30)
+        top = jnp.max(scores, axis=1, keepdims=True)
+        weight = jnp.where(valid, jnp.exp(scores - top), 0.0)
+        top_p[j] = top
+        total_p[j] = jnp.sum(weight, axis=1, keepdims=True)
+        summed_p[j] = dot(weight.astype(BF16), vp[...])
+        return carry
+
     def attend(j, carry):
         pick = pl.ds(pl.multiple_of(j * seqs, seqs), seqs)
-        q2 = jnp.concatenate(
-            [qt[:, pick, pl.ds(h * HEAD_DIM, HEAD_DIM)].reshape(nx * seqs, HEAD_DIM) for h in range(2)], axis=0
-        )
-        sp = jnp.where(valid, nt(q2, kp[...]) * scale, -1e30)
-        sd = jnp.where(own, nt(q2, dkv[:, 0, pick].reshape(nx * seqs, HEAD_DIM)) * scale, -1e30)
-        top = jnp.maximum(jnp.max(sp, axis=1, keepdims=True), jnp.max(sd, axis=1, keepdims=True))
-        wp = jnp.where(valid, jnp.exp(sp - top), 0.0)
-        wd = jnp.where(own, jnp.exp(sd - top), 0.0)
-        total = jnp.sum(wp, axis=1, keepdims=True) + jnp.sum(wd, axis=1, keepdims=True)
-        summed = dot(wp.astype(BF16), vp[...])
-        summed = summed + dot(wd.astype(BF16), dkv[:, 1, pick].reshape(nx * seqs, HEAD_DIM))
+        scores = nt(asked(pick), dkv[:, 0, pick].reshape(nx * seqs, HEAD_DIM)) * scale
+        scores = jnp.where(own, scores, -1e30)
+        top = jnp.maximum(top_p[j], jnp.max(scores, axis=1, keepdims=True))
+        weight = jnp.where(own, jnp.exp(scores - top), 0.0)
+        decay = jnp.exp(top_p[j] - top)
+        total = total_p[j] * decay + jnp.sum(weight, axis=1, keepdims=True)
+        summed = summed_p[j] * decay
+        summed = summed + dot(weight.astype(BF16), dkv[:, 1, pick].reshape(nx * seqs, HEAD_DIM))
         result = (summed / total).astype(BF16)
         for h in range(2):
             att[:, pick, pl.ds(h * HEAD_DIM, HEAD_DIM)] = result[h * nx * seqs:(h + 1) * nx * seqs].reshape(
@@ -342,32 +410,60 @@
             )
         return carry
 
-    lax.fori_loop(0, rows // seqs, attend, 0)
+    with jax.named_scope("straight#h=2"):
+        events(straight, 2)
+    with jax.named_scope("rest#h=1"):
+        events(rest, 1)
+    with jax.named_scope("attend_prompt"):
+        lax.fori_loop(0, rows // seqs // 2, functools.partial(twice, attend_prompt), 0)
+    with jax.named_scope("near#h=2"):
+        events(near, 2)
+    with jax.named_scope("kv_wait"):
+        ref = dkv.at[pl.ds(0, nx - 1)]
+        pltpu.make_async_copy(ref, ref, xs.at[1]).wait()
+        pltpu.make_async_copy(ref, ref, xr.at[1]).wait()
+    with jax.named_scope("attend"):
+        lax.fori_loop(0, rows // seqs // 2, functools.partial(twice, attend), 0)
+    with jax.named_scope("straight#h=3"):
+        events(straight, 3)
     for i in range(1, nx):
         to = lax.rem(x + i, nx)
         pltpu.make_async_remote_copy(
             att.at[to], full.at[x], xs.at[3], xr.at[3], device_id=(g, e, to), device_id_type=MESH
         ).start()
     full[x] = att[x]
-    for h in range(2, 5):
-        for ring in ow_y:
-            ring.event(h)
-    ref = full.at[pl.ds(0, nx - 1)]
-    pltpu.make_async_copy(ref, ref, xs.at[3]).wait()
-    pltpu.make_async_copy(ref, ref, xr.at[3]).wait()
-    mate_done(ow.at[pl.ds(0, nx), pl.ds(0, ny * orow)], 2)
+    with jax.named_scope("near#h=3"):
+        events(near, 3)
+    with jax.named_scope("rest#h=2"):
+        events(rest, 2)
+    with jax.named_scope("near#h=4"):
+        events(near, 4)
+    with jax.named_scope("rest#h=3"):
+        events(rest, 3)
+    with jax.named_scope("straight#h=4"):
+        events(straight, 4)
+    with jax.named_scope("rest#h=4"):
+        events(rest, 4)
+    with jax.named_scope("full_wait"):
+        ref = full.at[pl.ds(0, nx - 1)]
+        pltpu.make_async_copy(ref, ref, xs.at[3]).wait()
+        pltpu.make_async_copy(ref, ref, xr.at[3]).wait()
+    with jax.named_scope("ow_mate"):
+        mate_done(ow.at[pl.ds(0, nx), pl.ds(0, ny * orow), spread_cols], 1)
+        mate_done(ow.at[pl.ds(0, nx - 1), pl.ds(0, 2 * lines), pl.ds(0, DIRECT)], 4)
 
     tile = 512
 
     def project(i, carry):
         cols = pl.ds(pl.multiple_of(i * tile, tile), tile)
-        total = dot(full[0], ow[0, :, cols])
+        total = dot(full[x], ow[FAR, :, cols])
         for k in range(1, nx):
-            total = total + dot(full[k], ow[k, :, cols])
+            total = total + dot(full[lax.rem(x + k, nx)], ow[(FAR + k) % nx, :, cols])
         mixed_ref[:, cols] = (hidden_ref[:, cols].astype(F32) + total).astype(BF16)
         return carry
 
-    lax.fori_loop(0, width // tile, project, 0)
+    with jax.named_scope("project"):
+        lax.fori_loop(0, width // tile, project, 0)
     lane = lax.broadcasted_iota(jnp.int32, (rows, rows), 1)
     line = lax.broadcasted_iota(jnp.int32, (rows, rows), 0)
     idcol = jnp.sum(jnp.where(lane == line, idrow_ref[...], 0), axis=1, keepdims=True)
@@ -492,7 +588,7 @@
 
         with jax.named_scope("combine"):
             tiles(chunk, combine)
-    for ring in kv_x + kv_y + ow_x + ow_y:
+    for ring in kv_x + kv_y + ow_x + near + rest + straight:
         ring.finish()
 
 
@@ -537,11 +633,14 @@
             pltpu.VMEM((nx, rows, cols), BF16),
             pltpu.VMEM((nx, rows, cols), BF16),
             pltpu.VMEM((rows, width), BF16),
+            pltpu.VMEM((rows // 16, 32 * nx, 1), F32),
+            pltpu.VMEM((rows // 16, 32 * nx, 1), F32),
+            pltpu.VMEM((rows // 16, 32 * nx, HEAD_DIM), F32),
             pltpu.VMEM(gate.shape, BF16), pltpu.VMEM(up.shape, BF16), pltpu.VMEM(down.shape, BF16),
             pltpu.VMEM((rows, width), BF16), pltpu.VMEM((2 * nx * ne, ff), BF16),
             pltpu.VMEM((2 * nx * ne, ff), F32), pltpu.VMEM((2 * nx * ne, ff), F32),
             xe, ex, xe, ex, ex, xe, ex, xe, ex, xe, ex, xe, xe, ex, xe, ex,
-            sem((7,)), sem((3,)), sem((16,)), sem((16, 4)), sem((4,)), sem((4,)), sem((4,)), sem((4,)),
+            sem((8,)), sem((3,)), sem((22,)), sem((22, 4)), sem((5,)), sem((5,)), sem((4,)), sem((4,)),
             sem((8, CHUNKS)), sem((8, CHUNKS)),
         ],
         compiler_params=pltpu.CompilerParams(

time: 159 us -> 147 us (0.925)
  Pallas kernels: 157 us -> 145 us
    pallas_call x1, Pallas kernels: 157 us -> 145 us  [layer(): pl.pallas_call(functools.partial(layer_kernel, nx, ne), out_shape=jax.Sha...]
where the time goes in v4:
time: 147 us
  Pallas kernels  145 us (99%)
  local copies, waits for them, and re-layouts  1.88 us (1%)
    pallas_call x1, Pallas kernels, layer(): pl.pallas_call(functools.partial(layer_kernel, nx, ne), out_shape=jax.Sha...  145 us

profile of v4, /device:TPU:513, one launch (start us, length us, event | category | flops | bytes accessed | tf_op | source)
XLA Modules:
  0.0 147.1 jit_solution(9147171499083282435)
XLA Ops:
  0.0 145.2 %layer.1 = bf16[128,2048]{1,0:T(8,128)(2,1)} custom-call(bf16[96,2048]{1,0:T(8,128)(2,1)} %bitcast.19, bf16[128,2048]{1,0:T(8,128)(2,1)} %bitcast.17, bf16[1024,256]{1,0:T(8,128)(2,1)} %bitcast.18, f32[1,2048]{1,0:T(1,128)} %bitcast.20, f32[1,2048]{1,0:T(1,128)} %bitcast.21, s32[4]{0:T(128)} %lengths_ref.1, s32[128]{0:T(128)} %bitcast.22, ...), custom_call_target="tpu_custom_call" | custom-call | tf_op jit(solution)/shard_map/layer/pallas_call | solution.py:609
  145.2 1.9 %copy.15 = bf16[128,1,2048]{2,0,1:T(8,128)(2,1)} copy(bf16[128,1,2048]{2,0,1:T(8,128)(2,1)} %bitcast.15) | data formatting | bytes 1048576

commit v5 on v4

--- a/solution.py
+++ b/solution.py
@@ -36,7 +36,7 @@
 SHARED_ROWS = 1024
 DIRECT = 512
 FAR = 4
-CHUNKS = 2
+CHUNKS = 4
 
 
 def layer_kernel(

time: 147 us -> 145 us (0.986)
  Pallas kernels: 145 us -> 143 us
    pallas_call x1, Pallas kernels: 145 us -> 143 us  [layer(): pl.pallas_call(functools.partial(layer_kernel, nx, ne), out_shape=jax.Sha...]
where the time goes in v5:
time: 145 us
  Pallas kernels  143 us (99%)
  local copies, waits for them, and re-layouts  1.88 us (1%)
    pallas_call x1, Pallas kernels, layer(): pl.pallas_call(functools.partial(layer_kernel, nx, ne), out_shape=jax.Sha...  143 us

profile of v5, /device:TPU:513, one launch (start us, length us, event | category | flops | bytes accessed | tf_op | source)
XLA Modules:
  0.0 144.9 jit_solution(15654587205254320660)
XLA Ops:
  0.0 143.0 %layer.1 = bf16[128,2048]{1,0:T(8,128)(2,1)} custom-call(bf16[96,2048]{1,0:T(8,128)(2,1)} %bitcast.19, bf16[128,2048]{1,0:T(8,128)(2,1)} %bitcast.17, bf16[1024,256]{1,0:T(8,128)(2,1)} %bitcast.18, f32[1,2048]{1,0:T(1,128)} %bitcast.20, f32[1,2048]{1,0:T(1,128)} %bitcast.21, s32[4]{0:T(128)} %lengths_ref.1, s32[128]{0:T(128)} %bitcast.22, ...), custom_call_target="tpu_custom_call" | custom-call | tf_op jit(solution)/shard_map/layer/pallas_call | solution.py:609
  143.0 1.9 %copy.15 = bf16[128,1,2048]{2,0,1:T(8,128)(2,1)} copy(bf16[128,1,2048]{2,0,1:T(8,128)(2,1)} %bitcast.15) | data formatting | bytes 1048576

commit v6 on v5

--- a/solution.py
+++ b/solution.py
@@ -410,12 +410,12 @@
             )
         return carry
 
-    with jax.named_scope("straight#h=2"):
-        events(straight, 2)
     with jax.named_scope("rest#h=1"):
         events(rest, 1)
     with jax.named_scope("attend_prompt"):
         lax.fori_loop(0, rows // seqs // 2, functools.partial(twice, attend_prompt), 0)
+    with jax.named_scope("straight#h=2"):
+        events(straight, 2)
     with jax.named_scope("near#h=2"):
         events(near, 2)
     with jax.named_scope("kv_wait"):

time: 145 us -> 145 us (level)
  no operation moved by 1% of the time
where the time goes in v6:
time: 145 us
  Pallas kernels  143 us (99%)
  local copies, waits for them, and re-layouts  1.88 us (1%)
    pallas_call x1, Pallas kernels, layer(): pl.pallas_call(functools.partial(layer_kernel, nx, ne), out_shape=jax.Sha...  143 us

profile of v6, /device:TPU:513, one launch (start us, length us, event | category | flops | bytes accessed | tf_op | source)
XLA Modules:
  0.0 144.8 jit_solution(9481699007685588448)
XLA Ops:
  0.0 142.9 %layer.1 = bf16[128,2048]{1,0:T(8,128)(2,1)} custom-call(bf16[96,2048]{1,0:T(8,128)(2,1)} %bitcast.19, bf16[128,2048]{1,0:T(8,128)(2,1)} %bitcast.17, bf16[1024,256]{1,0:T(8,128)(2,1)} %bitcast.18, f32[1,2048]{1,0:T(1,128)} %bitcast.20, f32[1,2048]{1,0:T(1,128)} %bitcast.21, s32[4]{0:T(128)} %lengths_ref.1, s32[128]{0:T(128)} %bitcast.22, ...), custom_call_target="tpu_custom_call" | custom-call | tf_op jit(solution)/shard_map/layer/pallas_call | solution.py:609
  142.9 1.9 %copy.15 = bf16[128,1,2048]{2,0,1:T(8,128)(2,1)} copy(bf16[128,1,2048]{2,0,1:T(8,128)(2,1)} %bitcast.15) | data formatting | bytes 1048576
